TPU v7x, 32 devices: a whole 2x2x4 slice. The times are simulated.
32 devices in a mesh: dp: 2 (over core), seq: 8 (over z, y), head: 2 (over x).
Axes of the slice: x: 2, y: 2, z: 4, core: 2. Of those that a mesh axis runs over, the one named last changes fastest.
Arguments:
- hidden_in: bfloat16 [8, 1024, 1536], P('dp', 'seq'), may hold values from -6 to 6
- segment_ids: int32 [8, 1024], P('dp', 'seq'), may hold values from 0 to 6, as said below
- position_ids: int32 [8, 1024], P('dp', 'seq'), may hold values from 0 to 1017, as said below
- out_cot: bfloat16 [8, 1024, 1536], P('dp', 'seq'), may hold values from -6 to 6
- attn_gain: bfloat16 [1536], replicated, may hold values from 0.5 to 1.5
- w_query: bfloat16 [1536, 1536], P(('dp', 'seq'), 'head'), may hold values from -0.15625 to 0.15625
- b_query: bfloat16 [12, 128], P('head'), may hold values from -3 to 3
- w_key: bfloat16 [1536, 256], P(('dp', 'seq'), 'head'), may hold values from -0.15625 to 0.15625
- b_key: bfloat16 [2, 128], P('head'), may hold values from -3 to 3
- w_value: bfloat16 [1536, 256], P(('dp', 'seq'), 'head'), may hold values from -0.15625 to 0.15625
- b_value: bfloat16 [2, 128], P('head'), may hold values from -3 to 3
- w_out: bfloat16 [1536, 1536], P('head', ('dp', 'seq')), may hold values from -0.625 to 0.625
- ffn_gain: bfloat16 [1536], replicated, may hold values from 0.5 to 1.5
- w_gate: bfloat16 [1536, 8960], P(('dp', 'seq'), 'head'), may hold values from -0.15625 to 0.15625
- w_up: bfloat16 [1536, 8960], P(('dp', 'seq'), 'head'), may hold values from -0.15625 to 0.15625
- w_down: bfloat16 [8960, 1536], P('head', ('dp', 'seq')), may hold values from -0.125 to 0.125
Outputs:
- layer_out: bfloat16 [8, 1024, 1536], P('dp', 'seq')
- input_grad: bfloat16 [8, 1024, 1536], P('dp', 'seq')
- grad_attn_gain: float32 [1536], P(('dp', 'seq'))
- grad_w_query: float32 [1536, 1536], P(('dp', 'seq'), 'head')
- grad_b_query: float32 [12, 128], P('head', ('dp', 'seq'))
- grad_w_key: float32 [1536, 256], P(('dp', 'seq'), 'head')
- grad_b_key: float32 [2, 128], P('head')
- grad_w_value: float32 [1536, 256], P(('dp', 'seq'), 'head')
- grad_b_value: float32 [2, 128], P('head', ('dp', 'seq'))
- grad_w_out: float32 [1536, 1536], P('head', ('dp', 'seq'))
- grad_ffn_gain: float32 [1536], P(('dp', 'seq'))
- grad_w_gate: float32 [1536, 8960], P(('dp', 'seq'), 'head')
- grad_w_up: float32 [1536, 8960], P(('dp', 'seq'), 'head')
- grad_w_down: float32 [8960, 1536], P('head', ('dp', 'seq'))
Inputs may be any that keep to these rules, and one draw needn't show every extreme that they name: `segment_ids`: each row's 1024 positions are stored in blocks of 128: block number b holds the row's natural positions b * 64 to b * 64 + 63, then 1024 - (b + 1) * 64 to 1024 - b * 64 - 1, each in rising order. In natural order a row holds 6 documents of uneven lengths with ids 1 to 6, rising, then one or more padding positions with id 0. `position_ids`: in natural order (stored as for segment_ids) the ids count 0, 1, 2 and so on from the start of each document and of the padding.
All inputs are finite; a program needn't handle non-finite values.
Results may differ from a plain program's by a relative error of at most 0.024.
Values may be sent and summed in bfloat16 or wider, within the bound.
A program may use at most 256 MiB of HBM per device.

v0:
```python
import functools

import jax
import jax.numpy as jnp
from jax import lax
from jax.experimental import pallas as pl
from jax.experimental.pallas import tpu as pltpu
from jax.sharding import PartitionSpec as P


EPSILON = 1e-06
THETA = 1000000.0
MASKED = -1e30
LANES = 128
BF16 = jnp.bfloat16
F32 = jnp.float32
MESH = pl.DeviceIdType.MESH


def rope_tables(position, head_size):
    half_size = head_size // 2
    frequency = THETA ** (-jnp.arange(half_size, dtype=F32) * 2.0 / head_size)
    angles = position.astype(F32)[:, None] * frequency[None, :]
    return jnp.cos(angles), jnp.sin(angles)


def rotate(values, cosine, sine_table, direction):
    half_size = values.shape[-1] // 2
    first_half = values[..., :half_size]
    second_half = values[..., half_size:]
    return jnp.concatenate(
        [
            first_half * cosine - direction * (second_half * sine_table),
            second_half * cosine + direction * (first_half * sine_table),
        ],
        axis=-1,
    )


def xor(index, mask):
    out = index
    bit = 1
    while bit <= mask:
        if mask & bit:
            out = out + bit - 2 * bit * lax.rem(lax.div(index, bit), 2)
        bit *= 2
    return out


def plain_dot(left, right):
    return jnp.dot(left, right, preferred_element_type=F32)


def grad_of_weight(left, right):
    return lax.dot_general(left, right, (((0,), (0,)), ((), ())), preferred_element_type=F32)


def through_weight(left, right):
    return lax.dot_general(left, right, (((1,), (1,)), ((), ())), preferred_element_type=F32)


def norm_scale(values):
    return lax.rsqrt(jnp.mean(values * values, axis=-1, keepdims=True) + EPSILON)


def norm_back(grad_in, values, scale_rows, gain):
    scaled = grad_in * gain
    cubed = scale_rows * scale_rows * scale_rows
    return scale_rows * scaled - values * cubed * jnp.mean(scaled * values, axis=-1, keepdims=True)


def flip(values, axis, mask):
    size = lax.axis_size(axis)
    return lax.ppermute(values, axis, [(i, i ^ mask) for i in range(size)])


def after(values, gate):
    return lax.optimization_barrier((values, gate))[0]


def take(buffer, index, axis=0):
    return lax.dynamic_index_in_dim(buffer, index, axis, keepdims=False)


def allowed_keys(seg_q, pos_q, seg_k, pos_k):
    return (seg_q == seg_k) & (pos_k <= pos_q)


def dot_nt(left, right):
    return lax.dot_general(left, right, (((1,), (1,)), ((), ())), preferred_element_type=F32)


def dot_tn(left, right):
    return lax.dot_general(left, right, (((0,), (0,)), ((), ())), preferred_element_type=F32)


def probabilities(query, keys, allowed, factor):
    scores = jnp.where(allowed, dot_nt(query, keys) * factor, MASKED)
    top = jnp.max(scores, axis=-1, keepdims=True)
    terms = jnp.where(allowed, jnp.exp(scores - top), 0.0)
    return terms / jnp.sum(terms, axis=-1, keepdims=True)


def attend_kernel(heads, head_size, factor, q_ref, kv_ref, sq_ref, pq_ref, sk_ref, pk_ref, o_ref):
    allowed = allowed_keys(sq_ref[0], pq_ref[0], sk_ref[0], pk_ref[0])
    joint = kv_ref[:, 0].reshape(-1, 2 * head_size)
    keys = joint[:, :head_size]
    values = joint[:, head_size:]
    for head in range(heads):
        lanes = slice(head * head_size, (head + 1) * head_size)
        probs = probabilities(q_ref[0, :, lanes], keys, allowed, factor)
        o_ref[0, :, lanes] = jnp.dot(
            probs.astype(BF16), values, preferred_element_type=F32
        ).astype(BF16)


def attend_back_kernel(
    heads, head_size, factor, q_ref, do_ref, kv_ref, sq_ref, pq_ref, sk_ref, pk_ref,
    cos_ref, sin_ref, dq_ref, dkv_ref, acc
):
    allowed = allowed_keys(sq_ref[0], pq_ref[0], sk_ref[0], pk_ref[0])
    joint = kv_ref[:, 0].reshape(-1, 2 * head_size)
    keys = joint[:, :head_size]
    values = joint[:, head_size:]
    for head in range(heads):
        lanes = slice(head * head_size, (head + 1) * head_size)
        query = q_ref[0, :, lanes]
        d_out = do_ref[0, :, lanes]
        probs = probabilities(query, keys, allowed, factor)
        d_probs = dot_nt(d_out, values)
        delta = jnp.sum(probs * d_probs, axis=-1, keepdims=True)
        d_scores = (probs * (d_probs - delta)).astype(BF16)
        d_query = jnp.dot(d_scores, keys, preferred_element_type=F32) * factor
        turned = pltpu.roll(d_query, head_size // 2, 1)
        dq_ref[0, :, lanes] = (d_query * cos_ref[0] + turned * sin_ref[0]).astype(BF16)
        d_key = dot_tn(d_scores, query) * factor
        d_value = dot_tn(probs.astype(BF16), d_out)
        if head == 0:
            acc[:, :head_size] = d_key
            acc[:, head_size:] = d_value
        else:
            acc[:, :head_size] += d_key
            acc[:, head_size:] += d_value
    dkv_ref[:, 0] = acc[...].astype(BF16).reshape(dkv_ref.shape[0], -1, 2 * head_size)


def row_spec(*shape):
    return pl.BlockSpec((1,) + shape, lambda row: (row,) + (0,) * len(shape))


def keys_spec(places, *shape):
    return pl.BlockSpec(
        (places, 1) + shape, lambda row: (0, row) + (0,) * len(shape)
    )


def attend(queries, all_kv, marks, heads, head_size, factor):
    rows, width, wide = queries.shape
    places = all_kv.shape[0]
    length = places * width
    return pl.pallas_call(
        functools.partial(attend_kernel, heads, head_size, factor),
        grid=(rows,),
        out_shape=jax.ShapeDtypeStruct((rows, width, wide), BF16),
        in_specs=[
            row_spec(width, wide),
            keys_spec(places, width, 2 * head_size),
            row_spec(width, 1),
            row_spec(width, 1),
            row_spec(1, length),
            row_spec(1, length),
        ],
        out_specs=row_spec(width, wide),
        cost_estimate=pl.CostEstimate(
            flops=4 * rows * width * wide * length,
            bytes_accessed=4 * rows * (width * wide + length * head_size),
            transcendentals=rows * width * heads * length,
        ),
        name="attend",
    )(queries, all_kv, *marks)


def attend_back(queries, d_mixed, all_kv, marks, turns, heads, head_size, factor):
    rows, width, wide = queries.shape
    places = all_kv.shape[0]
    length = places * width
    return pl.pallas_call(
        functools.partial(attend_back_kernel, heads, head_size, factor),
        grid=(rows,),
        out_shape=(
            jax.ShapeDtypeStruct((rows, width, wide), BF16),
            jax.ShapeDtypeStruct((places, rows, width, 2 * head_size), BF16),
        ),
        in_specs=[
            row_spec(width, wide),
            row_spec(width, wide),
            keys_spec(places, width, 2 * head_size),
            row_spec(width, 1),
            row_spec(width, 1),
            row_spec(1, length),
            row_spec(1, length),
            row_spec(width, head_size),
            row_spec(width, head_size),
        ],
        out_specs=(row_spec(width, wide), keys_spec(places, width, 2 * head_size)),
        scratch_shapes=[pltpu.VMEM((length, 2 * head_size), F32)],
        cost_estimate=pl.CostEstimate(
            flops=10 * rows * width * wide * length,
            bytes_accessed=8 * rows * (width * wide + length * head_size),
            transcendentals=rows * width * heads * length,
        ),
        name="attend_back",
    )(queries, d_mixed, all_kv, *marks, *turns)


def partners_of(core, place, head, planes, over_core):
    found = [(core, xor(place, 2 * k), head) for k in range(1, planes)]
    found.append((core, xor(place, 1), head))
    if over_core:
        found.append((1 - core, place, head))
    return found


def greet(partners):
    barrier = pltpu.get_barrier_semaphore()
    for device in partners:
        pl.semaphore_signal(barrier, inc=1, device_id=device, device_id_type=MESH)
    pl.semaphore_wait(barrier, len(partners))


def remote(source, target, send_sem, recv_sem, device):
    copy = pltpu.make_async_remote_copy(
        src_ref=source,
        dst_ref=target,
        send_sem=send_sem,
        recv_sem=recv_sem,
        device_id=device,
        device_id_type=MESH,
    )
    copy.start()
    return copy


def quarter_start(which, block, units):
    return pl.multiple_of(which * block - lax.div(which, 3) * (4 * block - units), LANES)


def gather_kernel(places, flags, extra, block, normed, *refs):
    count = len(flags)
    sources, refs = refs[:count], refs[count:]
    weights, refs = refs[:extra], refs[extra:]
    if normed:
        (hidden_ref, gain_ref), refs = refs[:2], refs[2:]
    outs, refs = refs[:count], refs[count:]
    nears, refs = refs[:extra], refs[extra:]
    if normed:
        normed_ref, refs = refs[0], refs[1:]
    own_sem, send_z, recv_z, send_y, recv_y, send_c, recv_c, send_q, recv_q = refs
    core, place, head = lax.axis_index("dp"), lax.axis_index("seq"), lax.axis_index("head")
    planes = places // 2

    def slot(n, mask):
        where = xor(place, mask)
        return outs[n].at[core * places + where if flags[n] else where]

    partners = partners_of(core, place, head, planes, any(flags))
    if extra:
        partners.append((1 - core, xor(place, 2), head))
    greet(partners)
    near = (core, xor(place, 1), head)
    other = (1 - core, place, head)
    along, across, over, quarter = {}, {}, {}, {}
    for n in range(count):
        for k in range(1, planes):
            along[n, k] = remote(
                sources[n],
                slot(n, 0),
                send_z.at[n, k],
                recv_z.at[n, k],
                (core, xor(place, 2 * k), head),
            )
    local = []
    for n in range(count):
        across[n, 0] = remote(
            sources[n], slot(n, 0), send_y.at[n, 0], recv_y.at[n, 0], near
        )
        if flags[n]:
            over[n, 0] = remote(
                sources[n], slot(n, 0), send_c.at[n, 0], recv_c.at[n, 0], other
            )
        copy = pltpu.make_async_copy(sources[n], slot(n, 0), own_sem.at[n])
        copy.start()
        local.append(copy)
    for n in range(extra):
        units = weights[n].shape[1]
        for m in range(4):
            to_core = core if m % 2 == 0 else 1 - core
            to_place = xor(place, m // 2 * 2)
            which = lax.rem(lax.div(to_place, 2), 2) * 2 + to_core
            piece = weights[n].at[:, pl.ds(quarter_start(which, block, units), block)]
            if m:
                quarter[n, m] = remote(
                    piece,
                    nears[n].at[m],
                    send_q.at[n, m],
                    recv_q.at[n, m],
                    (to_core, to_place, head),
                )
            else:
                copy = pltpu.make_async_copy(piece, nears[n].at[0], send_q.at[n, 0])
                copy.start()
                local.append(copy)
    if normed:
        for row in range(hidden_ref.shape[0]):
            values = hidden_ref[row].astype(F32)
            normed_ref[row] = (values * norm_scale(values) * gain_ref[...]).astype(BF16)
    for n in range(count):
        for k in range(1, planes):
            along[n, k].wait_recv()
            piece = slot(n, 2 * k)
            across[n, k] = remote(piece, piece, send_y.at[n, k], recv_y.at[n, k], near)
            if flags[n]:
                over[n, 2 * k] = remote(
                    piece, piece, send_c.at[n, 2 * k], recv_c.at[n, 2 * k], other
                )
    for n in range(count):
        for k in range(planes):
            across[n, k].wait_recv()
            if flags[n]:
                mask = 2 * k + 1
                piece = slot(n, mask)
                over[n, mask] = remote(
                    piece, piece, send_c.at[n, mask], recv_c.at[n, mask], other
                )
    for copies in (over, quarter):
        for copy in copies.values():
            copy.wait_recv()
    for copies in (along, across, over, quarter):
        for copy in copies.values():
            copy.wait_send()
    for copy in local:
        copy.wait()


def gather_pieces(pieces, flags, ident, weights=(), block=0, norm=None):
    places = lax.axis_size("seq")
    planes = places // 2
    count, extra = len(pieces), len(weights)
    out_shape = [
        jax.ShapeDtypeStruct(((1 + flag) * places,) + piece.shape, piece.dtype)
        for piece, flag in zip(pieces, flags)
    ]
    out_shape += [jax.ShapeDtypeStruct((4, w.shape[0], block), w.dtype) for w in weights]
    out_specs = [pl.BlockSpec(memory_space=pl.ANY)] * (count + extra)
    operands = list(pieces) + list(weights)
    if norm is not None:
        operands += list(norm)
        out_shape.append(jax.ShapeDtypeStruct(norm[0].shape, BF16))
        out_specs.append(pl.BlockSpec(memory_space=pltpu.VMEM))
    quarters = (max(extra, 1), 4)
    return pl.pallas_call(
        functools.partial(gather_kernel, places, flags, extra, block, norm is not None),
        out_shape=tuple(out_shape),
        in_specs=[pl.BlockSpec(memory_space=pltpu.VMEM)] * len(operands),
        out_specs=tuple(out_specs),
        scratch_shapes=[
            pltpu.SemaphoreType.DMA((count,)),
            pltpu.SemaphoreType.DMA((count, planes)),
            pltpu.SemaphoreType.DMA((count, planes)),
            pltpu.SemaphoreType.DMA((count, planes)),
            pltpu.SemaphoreType.DMA((count, planes)),
            pltpu.SemaphoreType.DMA((count, places)),
            pltpu.SemaphoreType.DMA((count, places)),
            pltpu.SemaphoreType.DMA(quarters),
            pltpu.SemaphoreType.DMA(quarters),
        ],
        compiler_params=pltpu.CompilerParams(collective_id=ident, has_side_effects=True),
        cost_estimate=pl.CostEstimate(flops=0, bytes_accessed=100_000_000, transcendentals=0),
    )(*operands)


def reduce_kernel(places, flags, vector, first_row, extra, block, *refs):
    count = len(flags)
    planes = places // 2
    step = count + vector
    grads, refs = refs[:step], refs[step:]
    pieces, refs = refs[:extra], refs[extra:]
    totals, refs = refs[:step], refs[step:]
    wholes, refs = refs[:extra], refs[extra:]
    sems, refs = refs[:8], refs[8:]
    send_c, recv_c, send_y, recv_y, send_z, recv_z, send_q, recv_q = sems
    got_c, got_y, got_z, out_y, out_z = (refs[i * step : (i + 1) * step] for i in range(5))
    refs = refs[5 * step :]
    got_q, refs = refs[:extra], refs[extra:]
    core, place, head = lax.axis_index("dp"), lax.axis_index("seq"), lax.axis_index("head")
    level = lax.rem(lax.div(place, 2), 2)
    partners = partners_of(core, place, head, planes, any(flags))
    if extra:
        partners.append((1 - core, xor(place, 2), head))
    if vector:
        partners.append((core, place, 1 - head))
    greet(partners)
    near = (core, xor(place, 1), head)
    other = (1 - core, place, head)
    over, across, along, quarter = {}, {}, {}, {}
    order = [2 * k + 1 for k in range(planes)] + [2 * k for k in range(1, planes)] + [0]

    if vector:
        got_x, sum_x, sem_x = refs
        facing = remote(
            grads[count], got_x, sem_x.at[0], sem_x.at[1], (core, place, 1 - head)
        )
    for n in range(count):
        if flags[n]:
            for mask in order:
                over[n, mask] = remote(
                    grads[n].at[(1 - core) * places + xor(place, mask)],
                    got_c[n].at[mask],
                    send_c.at[n, mask],
                    recv_c.at[n, mask],
                    other,
                )
    for n in range(extra):
        for m in range(1, 4):
            to_core = core if m % 2 == 0 else 1 - core
            to_place = xor(place, m // 2 * 2)
            quarter[n, m] = remote(
                pieces[n].at[to_core, lax.rem(lax.div(to_place, 2), 2)],
                got_q[n].at[m],
                send_q.at[n, m],
                recv_q.at[n, m],
                (to_core, to_place, head),
            )

    def chip_sum(n, mask):
        where = xor(place, mask)
        if not flags[n]:
            return grads[n][where].astype(F32)
        over[n, mask].wait_recv()
        return grads[n][core * places + where].astype(F32) + got_c[n][mask].astype(F32)

    if vector:
        facing.wait_recv()
        rows = lax.broadcasted_iota(jnp.int32, got_x.shape, 0)
        sum_x[...] = grads[count][...] + jnp.where(rows >= first_row, got_x[...], 0.0)
        over[count, 0] = remote(
            sum_x, got_c[count], send_c.at[count, 0], recv_c.at[count, 0], other
        )
    for n in range(count):
        for k in list(range(1, planes)) + [0]:
            out_y[n][k] = chip_sum(n, 2 * k + 1).astype(BF16)
            across[n, k] = remote(
                out_y[n].at[k], got_y[n].at[k], send_y.at[n, k], recv_y.at[n, k], near
            )
    if vector:
        over[count, 0].wait_recv()
        out_y[count][...] = sum_x[...] + got_c[count][...]
        across[count, 0] = remote(
            out_y[count], got_y[count], send_y.at[count, 0], recv_y.at[count, 0], near
        )
    for n in range(extra):
        wholes[n][...] = jnp.zeros_like(wholes[n])
        units = wholes[n].shape[1]
        columns = pl.ds(quarter_start(level * 2 + core, block, units), block)
        wholes[n][:, columns] += pieces[n][core, level].astype(F32)
    for n in range(count):
        for k in range(1, planes):
            part = chip_sum(n, 2 * k)
            across[n, k].wait_recv()
            out_z[n][k] = (part + got_y[n][k].astype(F32)).astype(BF16)
            along[n, k] = remote(
                out_z[n].at[k],
                got_z[n].at[k],
                send_z.at[n, k],
                recv_z.at[n, k],
                (core, xor(place, 2 * k), head),
            )
    if vector:
        across[count, 0].wait_recv()
        out_z[count][...] = out_y[count][...] + got_y[count][...]
        for k in range(1, planes):
            along[count, k] = remote(
                out_z[count],
                got_z[count].at[k],
                send_z.at[count, k],
                recv_z.at[count, k],
                (core, xor(place, 2 * k), head),
            )
    for n in range(extra):
        units = wholes[n].shape[1]
        for m in range(1, 4):
            to_core = core if m % 2 == 0 else 1 - core
            which = (level if m < 2 else 1 - level) * 2 + to_core
            quarter[n, m].wait_recv()
            columns = pl.ds(quarter_start(which, block, units), block)
            wholes[n][:, columns] += got_q[n][m].astype(F32)
    for n in range(count):
        part = chip_sum(n, 0)
        across[n, 0].wait_recv()
        totals[n][...] = part + got_y[n][0].astype(F32)
    if vector:
        totals[count][...] = out_z[count][...]
    for n in range(step):
        for k in range(1, planes):
            along[n, k].wait_recv()
            totals[n][...] += got_z[n][k].astype(F32)
    if vector:
        facing.wait_send()
    for copies in (over, across, along, quarter):
        for copy in copies.values():
            copy.wait_send()


def reduce_pieces(grads, flags, vector, ident, first_row=0, pieces=(), units=0):
    places = lax.axis_size("seq")
    planes = places // 2
    count, extra = len(grads), len(pieces)
    shapes = [grad.shape[1:] for grad in grads]
    operands = list(grads)
    step = count
    if vector is not None:
        operands.append(vector)
        step += 1
    operands += list(pieces)
    block = pieces[0].shape[-1] if extra else 0
    small = (8, LANES)

    def buffers(leading, vector_leading):
        out = [pltpu.VMEM(leading + shape, BF16) for shape in shapes]
        if vector is not None:
            out.append(pltpu.VMEM(vector_leading + vector.shape, F32))
        return out

    got_c = [
        pltpu.VMEM(((places,) + shape) if flag else small, BF16)
        for shape, flag in zip(shapes, flags)
    ]
    if vector is not None:
        got_c.append(pltpu.VMEM(vector.shape, F32))
    quarters = (max(extra, 1), 4)
    scratch = (
        [
            pltpu.SemaphoreType.DMA((step, places)),
            pltpu.SemaphoreType.DMA((step, places)),
            pltpu.SemaphoreType.DMA((step, planes)),
            pltpu.SemaphoreType.DMA((step, planes)),
            pltpu.SemaphoreType.DMA((step, planes)),
            pltpu.SemaphoreType.DMA((step, planes)),
            pltpu.SemaphoreType.DMA(quarters),
            pltpu.SemaphoreType.DMA(quarters),
        ]
        + got_c
        + buffers((planes,), ())
        + buffers((planes,), (planes,))
        + buffers((planes,), ())
        + buffers((planes,), ())
        + [pltpu.VMEM((4,) + piece.shape[2:], BF16) for piece in pieces]
    )
    out_shapes = [jax.ShapeDtypeStruct(shape, F32) for shape in shapes]
    if vector is not None:
        scratch += [
            pltpu.VMEM(vector.shape, F32),
            pltpu.VMEM(vector.shape, F32),
            pltpu.SemaphoreType.DMA((2,)),
        ]
        out_shapes.append(jax.ShapeDtypeStruct(vector.shape, F32))
    out_shapes += [jax.ShapeDtypeStruct((piece.shape[2], units), F32) for piece in pieces]
    return pl.pallas_call(
        functools.partial(
            reduce_kernel, places, flags, int(vector is not None), first_row, extra, block
        ),
        out_shape=tuple(out_shapes),
        in_specs=[pl.BlockSpec(memory_space=pltpu.VMEM)] * len(operands),
        out_specs=tuple([pl.BlockSpec(memory_space=pltpu.VMEM)] * len(out_shapes)),
        scratch_shapes=scratch,
        compiler_params=pltpu.CompilerParams(collective_id=ident, has_side_effects=True),
        cost_estimate=pl.CostEstimate(flops=0, bytes_accessed=100_000_000, transcendentals=0),
    )(*operands)


def join_kernel(places, count, *refs):
    pieces, out, held, in_sem, out_sem = refs[:count], *refs[count:]
    core, place = lax.axis_index("dp"), lax.axis_index("seq")
    arriving = []
    for p in range(count):
        for q in range(4):
            i = 4 * p + q
            copy = pltpu.make_async_copy(pieces[p].at[q], held.at[i], in_sem.at[i])
            copy.start()
            arriving.append(copy)
    leaving = []
    for p in range(count):
        for q in range(4):
            i = 4 * p + q
            arriving[i].wait()
            mask = 4 * (p // 2) + 2 * (q // 2) + p % 2
            where = (core if q % 2 == 0 else 1 - core) * places + xor(place, mask)
            copy = pltpu.make_async_copy(held.at[i], out.at[where], out_sem.at[i])
            copy.start()
            leaving.append(copy)
    for copy in leaving:
        copy.wait()


def join_pieces(pieces):
    places = lax.axis_size("seq")
    count = len(pieces)
    _, rows, columns = pieces[0].shape
    total = 4 * count
    out = pl.pallas_call(
        functools.partial(join_kernel, places, count),
        out_shape=jax.ShapeDtypeStruct((total, rows, columns), BF16),
        in_specs=[pl.BlockSpec(memory_space=pl.ANY)] * count,
        out_specs=pl.BlockSpec(memory_space=pl.ANY),
        scratch_shapes=[
            pltpu.VMEM((total, rows, columns), BF16),
            pltpu.SemaphoreType.DMA((total,)),
            pltpu.SemaphoreType.DMA((total,)),
        ],
        cost_estimate=pl.CostEstimate(
            flops=0, bytes_accessed=4 * total * rows * columns, transcendentals=0
        ),
        name="join",
    )(*pieces)
    return out.reshape(total * rows, columns)


def sum_heads(part):
    low = lax.reduce_precision(part, 8, 7).astype(BF16)
    return low.astype(F32) + flip(low, "head", 1).astype(F32)


def in_order(own, other, head, axis):
    first = head == 0
    return jnp.concatenate(
        [jnp.where(first, own, other), jnp.where(first, other, own)], axis=axis
    )


def both_cores(values):
    return jnp.concatenate([values, flip(values, "dp", 1)], axis=0)


def far_rows(values, head):
    half = values.shape[0] // 2
    got = flip(lax.dynamic_slice_in_dim(values, head * half, half, 0), "seq", 2)
    return in_order(got, flip(got, "head", 1), head, 0)


def core_sum(part):
    half = part.shape[0] // 2
    return part[:half] + flip(part[half:].astype(BF16), "dp", 1).astype(F32)


def collect(near, far, pieces):
    far_low = core_sum(far).astype(BF16)
    near = core_sum(near)
    size = near.shape[0] // pieces
    out = []
    for i in range(pieces):
        rows = slice(i * size, (i + 1) * size)
        out.append(sum_heads(near[rows] + flip(far_low[rows], "seq", 2).astype(F32)))
    return jnp.concatenate(out, axis=0) if pieces > 1 else out[0]


def on_device(
    hidden_in,
    segment_ids,
    position_ids,
    out_cot,
    attn_gain,
    w_query,
    b_query,
    w_key,
    b_key,
    w_value,
    b_value,
    w_out,
    ffn_gain,
    w_gate,
    w_up,
    w_down,
):
    row_count, row_width, model_width = hidden_in.shape
    tokens = row_count * row_width
    heads, head_size = b_query.shape
    wide = heads * head_size
    factor = head_size ** (-0.5)
    places = lax.axis_size("seq")
    columns = places // 4
    core = lax.axis_index("dp")
    place = lax.axis_index("seq")
    head = lax.axis_index("head")
    column = place // 4
    level = (place // 2) % 2
    side = place % 2
    shard = w_gate.shape[0]
    units = w_gate.shape[1]
    block = -(-units // (4 * LANES)) * LANES

    gain_one = attn_gain.astype(F32)
    marks_own = jnp.concatenate([segment_ids, position_ids], axis=0)
    full_qkv, full_out, marks_all, near_gate, near_up, near_down, normed = gather_pieces(
        [jnp.concatenate([w_query, w_key, w_value], axis=1), w_out.T, marks_own],
        (1, 1, 0),
        0,
        (w_gate, w_up, w_down.T),
        block,
        (hidden_in, gain_one[None]),
    )
    normed = normed.reshape(tokens, model_width)
    full_qkv = full_qkv.reshape(model_width, -1)
    full_out = full_out.reshape(model_width, -1)
    marks_all = marks_all.reshape(places, 2, row_count, row_width).transpose(1, 2, 0, 3)
    marks_all = marks_all.reshape(2, row_count, 1, places * row_width)
    marks = (
        segment_ids[:, :, None],
        position_ids[:, :, None],
        marks_all[0],
        marks_all[1],
    )

    def column_gather(own):
        return [own] + [flip(own, "seq", 4 * k) for k in range(1, columns)]

    def side_gather(parts):
        pieces = []
        for part in parts:
            pieces += [part, flip(part, "seq", 1)]
        return join_pieces(pieces)

    gate_parts = column_gather(near_gate)

    hidden = hidden_in.reshape(tokens, model_width).astype(F32)
    scale_one = norm_scale(hidden)
    cosine, sine_table = rope_tables(position_ids.reshape(tokens), head_size)
    bias = jnp.concatenate([b_query.reshape(-1), b_key.reshape(-1), b_value.reshape(-1)])
    qkv = plain_dot(normed, full_qkv) + bias.astype(F32)
    queries = rotate(
        qkv[:, :wide].reshape(tokens, heads, head_size),
        cosine[:, None, :],
        sine_table[:, None, :],
        1.0,
    ).astype(BF16)
    queries = queries.reshape(row_count, row_width, wide)
    key_rot = rotate(qkv[:, wide : wide + head_size], cosine, sine_table, 1.0).astype(BF16)
    local_kv = jnp.concatenate([key_rot, qkv[:, wide + head_size :].astype(BF16)], axis=-1)
    local_kv = local_kv.reshape(row_count, row_width, 2 * head_size)
    (all_kv,) = gather_pieces([local_kv], (0,), 1)

    up_parts = column_gather(after(near_up, all_kv))
    full_gate = side_gather(gate_parts)
    full_up = side_gather(up_parts)

    out_other = flip(full_out, "head", 1)
    out_all = in_order(full_out, out_other, head, 1)

    mixed = attend(queries, all_kv, marks, heads, head_size, factor).reshape(tokens, wide)
    mixed_all = in_order(mixed, flip(mixed, "head", 1), head, 1)
    middle = hidden + through_weight(mixed_all, out_all)
    scale_two = norm_scale(middle)
    gain_two = ffn_gain.astype(F32)
    normed_own = (middle * scale_two * gain_two).astype(BF16)
    normed_far = far_rows(normed_own, head)

    down_parts = column_gather(after(near_down, normed_own))
    full_down = side_gather(down_parts)

    live_rows = (segment_ids != 0).astype(F32).reshape(tokens, 1)
    cotangent = out_cot.reshape(tokens, model_width).astype(F32) * live_rows
    cot_own = cotangent.astype(BF16)
    cot_far = far_rows(after(cot_own, normed_own), head)

    drawn_back = 4 * block - units
    live_units = (jnp.arange(block) >= drawn_back) | (level * 2 + core < 3)
    forward, backward, norms, cots = [], [], [], []
    for own_rows, own_cot in ((normed_own, cot_own), (normed_far, cot_far)):
        rows = both_cores(own_rows)
        gate_pre = jnp.where(live_units, plain_dot(rows, full_gate), 0.0)
        up_pre = jnp.where(live_units, plain_dot(rows, full_up), 0.0)
        sigmoid_gate = jax.nn.sigmoid(gate_pre)
        activated = gate_pre * sigmoid_gate
        product = (activated * up_pre).astype(BF16)
        cot_rows = both_cores(own_cot)
        d_product = plain_dot(cot_rows, full_down).astype(BF16).astype(F32)
        slope = sigmoid_gate * (1.0 + gate_pre * (1.0 - sigmoid_gate))
        d_gate = (d_product * up_pre * slope).astype(BF16)
        d_up = (d_product * activated).astype(BF16)
        norms.append(rows)
        cots.append(cot_rows)
        forward.append(product)
        backward.append((d_gate, d_up))
    back_parts = [
        through_weight(d_gate, full_gate) + through_weight(d_up, full_up)
        for d_gate, d_up in backward
    ]
    back_two = collect(*back_parts, 2)

    def weight_grad(lefts, rights):
        return (
            grad_of_weight(lefts[0], rights[0]) + grad_of_weight(lefts[1], rights[1])
        ).astype(BF16)

    grad_down = weight_grad(cots, forward)
    grad_gate = weight_grad(norms, [pair[0] for pair in backward])
    grad_up = weight_grad(norms, [pair[1] for pair in backward])
    result = middle + collect(*[through_weight(part, full_down) for part in forward], 1)
    layer_out = result.astype(BF16).reshape(row_count, row_width, model_width)

    ffn_sums = []
    for grad in (grad_down, grad_gate, grad_up):
        blocks = grad.reshape(2, columns, 2, 2, shard, block)
        half = take(blocks, side, 3).astype(F32)
        half = half + flip(take(blocks, 1 - side, 3), "seq", 1).astype(F32)
        low = half.astype(BF16)
        total = take(half, column, 1)
        for k in range(1, columns):
            total = total + flip(take(low, column ^ k, 1), "seq", 4 * k).astype(F32)
        ffn_sums.append(total.astype(BF16))

    gain_two_grad = jnp.sum(back_two * middle * scale_two, axis=0)
    d_middle = cotangent + norm_back(back_two, middle, scale_two, gain_two)
    d_middle_low = d_middle.astype(BF16)
    d_mixed = plain_dot(d_middle_low, full_out).astype(BF16)

    turns = (
        jnp.concatenate([cosine, cosine], axis=1).reshape(row_count, row_width, head_size),
        jnp.concatenate([sine_table, -sine_table], axis=1).reshape(
            row_count, row_width, head_size
        ),
    )
    d_query, d_kv_all = attend_back(
        queries,
        d_mixed.reshape(row_count, row_width, wide),
        all_kv,
        marks,
        turns,
        heads,
        head_size,
        factor,
    )
    (d_kv,) = reduce_pieces([d_kv_all], (0,), None, 2)
    d_kv = d_kv.reshape(tokens, 2 * head_size)
    d_key = rotate(d_kv[:, :head_size], cosine, sine_table, -1.0).astype(BF16)
    d_value = d_kv[:, head_size:].astype(BF16)
    d_qkv = jnp.concatenate([d_query.reshape(tokens, wide), d_key, d_value], axis=-1)
    back_part = through_weight(d_qkv, full_qkv)
    gain_one_part = jnp.sum(back_part * hidden * scale_one, axis=0)
    back_low = lax.reduce_precision(back_part, 8, 7).astype(BF16)
    back_other = after(flip(back_low, "head", 1), gain_one_part)
    back_one = back_low.astype(F32) + back_other.astype(F32)
    d_hidden = d_middle + norm_back(back_one, hidden, scale_one, gain_one)
    input_grad = d_hidden.astype(BF16).reshape(row_count, row_width, model_width)

    bias_grad = jnp.sum(d_qkv.astype(F32), axis=0)
    vectors = jnp.concatenate([bias_grad, gain_two_grad, gain_one_part])
    first_row = (vectors.size - model_width) // LANES
    qkv_grad = grad_of_weight(normed, d_qkv).astype(BF16).reshape(2 * places, shard, -1)
    out_grad = grad_of_weight(d_middle_low, mixed).astype(BF16).reshape(2 * places, shard, -1)
    qkv_sum, out_sum, vectors, down_sum, gate_sum, up_sum = reduce_pieces(
        [qkv_grad, out_grad], (1, 1), vectors.reshape(-1, LANES), 3, first_row, ffn_sums, units
    )
    out_sum = out_sum.T
    down_sum = down_sum.T
    vectors = vectors.reshape(-1)
    index = core * places + place
    replicas = 2 * places
    narrow = head_size // replicas
    bias_sums = vectors[: wide + 2 * head_size].reshape(heads + 2, head_size)
    bias_mine = lax.dynamic_slice_in_dim(bias_sums, index * narrow, narrow, 1)
    gains = vectors[wide + 2 * head_size :].reshape(2, replicas, model_width // replicas)
    gains_mine = take(gains, index, 1)
    return (
        layer_out,
        input_grad,
        gains_mine[1],
        qkv_sum[:, :wide],
        bias_mine[:heads],
        qkv_sum[:, wide : wide + head_size],
        bias_sums[heads : heads + 1],
        qkv_sum[:, wide + head_size :],
        bias_mine[heads + 1 :],
        out_sum,
        gains_mine[0],
        gate_sum,
        up_sum,
        down_sum,
    )


def solution(mesh):
    placed = (
        P("dp", "seq", None),
        P("dp", "seq"),
        P("dp", "seq"),
        P("dp", "seq", None),
        P(),
        P(("dp", "seq"), "head"),
        P("head", None),
        P(("dp", "seq"), "head"),
        P("head", None),
        P(("dp", "seq"), "head"),
        P("head", None),
        P("head", ("dp", "seq")),
        P(),
        P(("dp", "seq"), "head"),
        P(("dp", "seq"), "head"),
        P("head", ("dp", "seq")),
    )
    return jax.shard_map(
        on_device,
        mesh=mesh,
        in_specs=placed,
        out_specs=(
            P("dp", "seq", None),
            P("dp", "seq", None),
            P(("dp", "seq")),
            P(("dp", "seq"), "head"),
            P("head", ("dp", "seq")),
            P(("dp", "seq"), "head"),
            P("head", None),
            P(("dp", "seq"), "head"),
            P("head", ("dp", "seq")),
            P("head", ("dp", "seq")),
            P(("dp", "seq")),
            P(("dp", "seq"), "head"),
            P(("dp", "seq"), "head"),
            P("head", ("dp", "seq")),
        ),
        check_vma=False,
    )
```

profile of v0, /device:TPU:0, one launch (start us, length us, event | category | flops | bytes accessed | tf_op | source)
XLA Modules:
  0.0 833.0 jit_solution(3395353666347852191)
XLA Ops:
  4.9 61.0 %shard_map.263 = (bf16[16,96,1024]{2,1,0:T(8,128)(2,1)}, bf16[16,96,768]{2,1,0:T(8,128)(2,1)}, s32[8,8,128]{2,1,0:T(8,128)}, bf16[4,96,1152]{2,1,0:T(8,128)(2,1)...) custom-call(bf16[96,1024]{1,0:T(8,128)(2,1)} %pad_maximum_fusion.16.refs_0_, ...), custom_call_target="tpu_custom_call" | custom-call | bytes 100000000 | tf_op jit(solution)/shard_map/pallas_call | solution.py:361
  67.5 4.2 convolution_add_fusion.5
  79.2 35.1 %shard_map.264.kv_ref = bf16[8,4,128,256]{3,2,1,0:T(8,128)(2,1)} custom-call(bf16[4,128,256]{2,1,0:T(8,128)(2,1)} %bitcast.186), custom_call_target="tpu_custom_call" | custom-call | bytes 100000000 | tf_op jit(solution)/shard_map/pallas_call | solution.py:361
  114.9 14.1 %attend.1 = bf16[4,128,768]{2,1,0:T(8,128)(2,1)} custom-call(bf16[4,128,768]{2,1,0:T(8,128)(2,1)} %copy.56.q_ref, bf16[8,4,128,256]{3,2,1,0:T(8,128)(2,1)} %shard_map.264.kv_ref, s32[4,128,1]{2,1,0:T(8,128)} %copy.57.sq_ref, s32[4,128,1]{2,1,0:T(8,128)} %copy.58.pq_ref, s32[4,1,1024]{2,1,0:T(1,128)} %bitcast.201, s32[4,1,1024]{2,1,0:T(1,128)} %bitcast.199), custom_call_target="tpu_custom_call" | custom-call | flops 1610612736 | bytes 3670016 | tf_op jit(solution)/shard_map/attend/pallas_call | solution.py:161
  135.1 12.6 %collective-permute-done = bf16[512,768]{1,0:T(8,128)(2,1)S(1)} collective-permute-done((bf16[512,768]{1,0:T(8,128)(2,1)}, bf16[512,768]{1,0:T(8,128)(2,1)S(1)}, u32[]{:S(2)}, u32[]{:S(2)}) %collective-permute-start) | collective-permute-done | bytes 786464 | tf_op jit(solution)/shard_map/ppermute | solution.py:74
  151.0 38.5 %collective-permute-done.4.refs_2_ = bf16[4,96,1152]{2,1,0:T(8,128)(2,1)} collective-permute-done((bf16[4,96,1152]{2,1,0:T(8,128)(2,1)}, bf16[4,96,1152]{2,1,0:T(8,128)(2,1)}, u32[]{:S(2)}, u32[]{:S(2)}) %collective-permute-start.4) | collective-permute-done | bytes 884768 | tf_op jit(solution)/shard_map/ppermute | solution.py:74
  192.7 2.7 multiply_reduce_fusion.2
  200.4 7.6 collective-permute-done.7.refs_2_
  211.9 32.0 %collective-permute-done.13 = bf16[256,1536]{1,0:T(8,128)(2,1)} collective-permute-done((bf16[256,1536]{1,0:T(8,128)(2,1)S(1)}, bf16[256,1536]{1,0:T(8,128)(2,1)}, u32[]{:S(2)}, u32[]{:S(2)}) %collective-permute-start.13) | collective-permute-done | bytes 786464 | tf_op jit(solution)/shard_map/ppermute | solution.py:74
  248.5 3.6 join.3
  252.2 3.6 join.4
  256.9 3.8 collective-permute-done.21
  267.4 13.4 %collective-permute-done.22 = bf16[256,1536]{1,0:T(8,128)(2,1)S(1)} collective-permute-done((bf16[256,1536]{1,0:T(8,128)(2,1)}, bf16[256,1536]{1,0:T(8,128)(2,1)S(1)}, u32[]{:S(2)}, u32[]{:S(2)}) %collective-permute-start.22) | collective-permute-done | bytes 786464 | tf_op jit(solution)/shard_map/ppermute | solution.py:74
  284.8 7.8 convolution_select_fusion.3
  292.6 4.7 collective-permute-done.11.refs_3_
  297.3 3.6 join.5
  300.9 7.8 convolution_convert_fusion.2
  308.8 9.8 %fusion.4 = (bf16[1024,1152]{1,0:T(8,128)(2,1)}, bf16[1024,1152]{1,0:T(8,128)(2,1)S(1)}, bf16[1024,1152]{1,0:T(8,128)(2,1)}) fusion(bf16[1024,1152]{1,0:T(8,128)(2,1)S(1)} %convolution_convert_fusion.2, f32[1024,1152]{1,0:T(8,128)S(1)} %copy-done.62, bf16[1536,1152]{1,0:T(8,128)(2,1)S(1)} %bitcast.158, bf16[512,1536]{1,0:T(8,128)(2,1)S(1)} %copy-done.60, ...), kind=kOutput, calls=%fused_computation.11 | convolution fusion | flops 3650224128 | bytes 20841600 | tf_op jit(solution)/shard_map/dot_general | solution.py:51
  318.6 4.3 fusion.84
  326.2 4.2 fusion.86
  330.5 6.0 convolution_add_fusion.4
  339.0 8.3 convolution_convert_fusion.1
  347.3 6.0 convolution_select_fusion.1
  353.3 9.0 %fusion.7 = (bf16[1024,1152]{1,0:T(8,128)(2,1)}, bf16[1024,1152]{1,0:T(8,128)(2,1)}, bf16[1024,1152]{1,0:T(8,128)(2,1)}) fusion(bf16[1024,1152]{1,0:T(8,128)(2,1)S(1)} %copy-done.71, f32[1024,1152]{1,0:T(8,128)S(1)} %convolution_select_fusion.1, bf16[1536,1152]{1,0:T(8,128)(2,1)S(1)} %bitcast.160, bf16[512,1536]{1,0:T(8,128)(2,1)} %collective-permute-done.15, ...), kind=kOutput, calls=%fused_computation.14 | convolution fusion | flops 3653369856 | bytes 20841600 | tf_op jit(solution)/shard_map/dot_general | solution.py:51
  362.3 6.1 fusion.85
  368.4 9.9 %fusion.43 = f32[1536,1152]{1,0:T(8,128)} fusion(bf16[1024,1152]{1,0:T(8,128)(2,1)S(1)} %copy-done.65, bf16[512,1536]{1,0:T(8,128)(2,1)} %collective-permute-done.23, bf16[256,1536]{1,0:T(8,128)(2,1)S(1)} %copy-done.25, bf16[256,1536]{1,0:T(8,128)(2,1)S(1)} %copy-done.23), kind=kOutput, calls=%fused_computation.113 | convolution fusion | flops 3633315840 | bytes 12582912 | tf_op jit(solution)/shard_map/dot_general | solution.py:55
  378.4 8.6 %fusion = bf16[1536,1152]{1,0:T(8,128)(2,1)S(1)} fusion(f32[1536,1152]{1,0:T(8,128)} %fusion.43, bf16[1024,1152]{1,0:T(8,128)(2,1)S(1)} %copy-done.70, bf16[512,1536]{1,0:T(8,128)(2,1)} %collective-permute-done.19, bf16[512,1536]{1,0:T(8,128)(2,1)} %fusion.24), kind=kOutput, calls=%fused_computation.3 | convolution fusion | flops 3633709056 | bytes 16121856 | tf_op jit(solution)/shard_map/dot_general | solution.py:55
  390.9 4.3 fusion.87
  395.2 4.3 convolution_add_fusion.3
  400.3 9.7 %fusion.78 = f32[1536,1152]{1,0:T(8,128)} fusion(bf16[1024,1152]{1,0:T(8,128)(2,1)S(1)} %copy-done.64, bf16[512,1536]{1,0:T(8,128)(2,1)} %collective-permute-done.15, bf16[256,1536]{1,0:T(8,128)(2,1)S(1)} %copy-done.21, bf16[256,1536]{1,0:T(8,128)(2,1)S(1)} %copy-done.19), kind=kOutput, calls=%fused_computation.193 | convolution fusion | flops 3633315840 | bytes 12582912 | tf_op jit(solution)/shard_map/dot_general | solution.py:55
  410.0 9.0 %fusion.77 = f32[1536,1152]{1,0:T(8,128)} fusion(bf16[1024,1152]{1,0:T(8,128)(2,1)S(1)} %copy-done.63, bf16[512,1536]{1,0:T(8,128)(2,1)} %collective-permute-done.15, bf16[256,1536]{1,0:T(8,128)(2,1)S(1)} %copy-done.21, bf16[256,1536]{1,0:T(8,128)(2,1)S(1)} %copy-done.19), kind=kOutput, calls=%fused_computation.192 | convolution fusion | flops 3633315840 | bytes 12582912 | tf_op jit(solution)/shard_map/dot_general | solution.py:55
  419.0 8.0 fusion.1
  427.0 8.0 fusion.2
  448.9 28.6 %collective-permute-done.32 = bf16[2,2,2,96,1152]{4,3,2,0,1:T(8,128)(2,1)S(1)} collective-permute-done((bf16[2,2,2,96,1152]{4,3,2,0,1:T(8,128)(2,1)S(1)}, bf16[2,2,2,96,1152]{4,3,2,0,1:T(8,128)(2,1)S(1)}, u32[]{:S(2)}, u32[]{:S(2)}) %collective-permute-start.32) | collective-permute-done | bytes 1769504 | tf_op jit(solution)/shard_map/ppermute | solution.py:74
  477.8 36.6 %collective-permute-done.34 = bf16[2,2,2,96,1152]{4,3,2,0,1:T(8,128)(2,1)S(1)} collective-permute-done((bf16[2,2,2,96,1152]{4,3,2,0,1:T(8,128)(2,1)S(1)}, bf16[2,2,2,96,1152]{4,3,2,0,1:T(8,128)(2,1)S(1)}, u32[]{:S(2)}, u32[]{:S(2)}) %collective-permute-start.34) | collective-permute-done | bytes 1769504 | tf_op jit(solution)/shard_map/ppermute | solution.py:74
  515.9 2.9 collective-permute-start.33
  519.4 72.4 %collective-permute-done.31 = bf16[2,2,96,1152]{3,2,1,0:T(8,128)(2,1)S(1)} collective-permute-done((bf16[2,2,96,1152]{3,2,1,0:T(8,128)(2,1)S(1)}, bf16[2,2,96,1152]{3,2,1,0:T(8,128)(2,1)S(1)}, u32[]{:S(2)}, u32[]{:S(2)}) %collective-permute-start.31) | collective-permute-done | bytes 884768 | tf_op jit(solution)/shard_map/ppermute | solution.py:74
  593.5 17.3 %collective-permute-done.33 = bf16[2,2,96,1152]{3,2,1,0:T(8,128)(2,1)S(1)} collective-permute-done((bf16[2,2,96,1152]{3,2,1,0:T(8,128)(2,1)S(1)}, bf16[2,2,96,1152]{3,2,1,0:T(8,128)(2,1)S(1)}, u32[]{:S(2)}, u32[]{:S(2)}) %collective-permute-start.33) | collective-permute-done | bytes 884768 | tf_op jit(solution)/shard_map/ppermute | solution.py:74
  616.5 14.7 %collective-permute-done.28 = bf16[256,1536]{1,0:T(8,128)(2,1)S(1)} collective-permute-done((bf16[256,1536]{1,0:T(8,128)(2,1)S(1)}, bf16[256,1536]{1,0:T(8,128)(2,1)S(1)}, u32[]{:S(2)}, u32[]{:S(2)}) %collective-permute-start.28) | collective-permute-done | bytes 786464 | tf_op jit(solution)/shard_map/ppermute | solution.py:74
  632.3 31.6 %collective-permute-done.18 = bf16[512,1536]{1,0:T(8,128)(2,1)S(1)} collective-permute-done((bf16[512,1536]{1,0:T(8,128)(2,1)S(1)}, bf16[512,1536]{1,0:T(8,128)(2,1)S(1)}, u32[]{:S(2)}, u32[]{:S(2)}) %collective-permute-start.18) | collective-permute-done | bytes 1572896 | tf_op jit(solution)/shard_map/ppermute | solution.py:74
  663.9 3.0 fusion.23
  669.2 21.1 %attend_back.1 = (bf16[4,128,768]{2,1,0:T(8,128)(2,1)}, bf16[8,4,128,256]{3,2,1,0:T(8,128)(2,1)}) custom-call(bf16[4,128,768]{2,1,0:T(8,128)(2,1)} %copy.56.q_ref, bf16[4,128,768]{2,1,0:T(8,128)(2,1)} %bitcast.211, bf16[8,4,128,256]{3,2,1,0:T(8,128)(2,1)} %shard_map.264.kv_ref, s32[4,128,1]{2,1,0:T(8,128)} %copy.57.sq_ref, s32[4,128,1]{2,1,0:T(8,128)} %copy.58.pq_ref, ...), custom_call_target="tpu_custom_call" | custom-call | flops 4026531840 | bytes 7340032 | tf_op jit(solution)/shard_map/attend_back/pallas_call | solution.py:187
  690.3 36.5 %shard_map.265 = f32[4,128,256]{2,1,0:T(8,128)} custom-call(bf16[8,4,128,256]{3,2,1,0:T(8,128)(2,1)} %get-tuple-element.44.refs_0_), custom_call_target="tpu_custom_call" | custom-call | bytes 100000000 | tf_op jit(solution)/shard_map/pallas_call | solution.py:568
  730.1 4.2 fusion.26
  738.4 2.9 convolution_convert_fusion.3
  741.3 3.5 convolution_convert_fusion
  744.8 70.3 %shard_map.266 = (f32[96,1024]{1,0:T(8,128)}, f32[96,768]{1,0:T(8,128)}, f32[32,128]{1,0:T(8,128)}, f32[96,4480]{1,0:T(8,128)}, f32[96,4480]{1,0:T(8,128)}, /*index=5*/f32[96,4480]{1,0:T(8,128)}) custom-call(bf16[16,96,1024]{2,1,0:T(8,128)(2,1)} %bitcast.175, bf16[16,96,768]{2,1,0:T(8,128)(2,1)} %bitcast.180, f32[32,128]{1,0:T(8,128)} %maximum_bitcast_fusion.refs_2_, ...), custom_call_target="tpu_custom_call" | custom-call | bytes 100000000 | tf_op jit(solution)/shard_map/pallas_call | solution.py:568
  824.5 3.8 fusion.30
  (314 shorter events, 109.5 us)
Async XLA Ops:
  0.6 66.8 %copy-start.56 = (bf16[1,128]{1,0:T(2,128)(2,1)S(1)}, bf16[1,128]{1,0:T(2,128)(2,1)}, u32[]{:S(2)}) copy-start(bf16[1,128]{1,0:T(2,128)(2,1)} %param.26) | copy-start | bytes 772
  0.7 66.8 %copy-start.57 = (bf16[1,128]{1,0:T(2,128)(2,1)S(1)}, bf16[1,128]{1,0:T(2,128)(2,1)}, u32[]{:S(2)}) copy-start(bf16[1,128]{1,0:T(2,128)(2,1)} %param.24) | copy-start | bytes 772
  0.7 66.8 %copy-start.55 = (bf16[6,128]{1,0:T(8,128)(2,1)S(1)}, bf16[6,128]{1,0:T(8,128)(2,1)}, u32[]{:S(2)}) copy-start(bf16[6,128]{1,0:T(8,128)(2,1)} %param.22) | copy-start | bytes 4612
  65.9 124.1 %collective-permute-start.1 = (bf16[1536,768]{1,0:T(8,128)(2,1)}, bf16[1536,768]{1,0:T(8,128)(2,1)}, u32[]{:S(2)}, u32[]{:S(2)}) collective-permute-start(bf16[1536,768]{1,0:T(8,128)(2,1)} %bitcast.178), channel_id=1, source_target_pairs={{0,1},{1,0},{2,3},{3,2},{4,5},{5,4},{6,7},{7,6},{8,9},{9,8},{10,11... | collective-permute-start | bytes 7077896 | tf_op jit(solution)/shard_map/ppermute | solution.py:74
  74.9 59.2 %copy-start.51 = (f32[64]{0:T(128)}, f32[64]{0:T(128)S(1)}, u32[]{:S(2)}) copy-start(f32[64]{0:T(128)S(1)} %multiply_power_fusion) | copy-start | bytes 772
  129.0 18.7 %collective-permute-start = (bf16[512,768]{1,0:T(8,128)(2,1)}, bf16[512,768]{1,0:T(8,128)(2,1)S(1)}, u32[]{:S(2)}, u32[]{:S(2)}) collective-permute-start(bf16[512,768]{1,0:T(8,128)(2,1)} %bitcast.191), channel_id=1, source_target_pairs={{0,1},{1,0},{2,3},{3,2},{4,5},{5,4},{6,7},{7,6},{8,9},{9,8},{10,11... | collective-permute-start | bytes 2359304 | tf_op jit(solution)/shard_map/ppermute | solution.py:74
  129.6 59.9 %collective-permute-start.4 = (bf16[4,96,1152]{2,1,0:T(8,128)(2,1)}, bf16[4,96,1152]{2,1,0:T(8,128)(2,1)}, u32[]{:S(2)}, u32[]{:S(2)}) collective-permute-start(bf16[4,96,1152]{2,1,0:T(8,128)(2,1)} %get-tuple-element.37.refs_0_), channel_id=1, source_target_pairs={{0,8},{2,10},{4,12},{6,14},{8,0},{10,2},{12,4},{14,6},{1,9},{3,11}... | collective-permute-start | bytes 2654216 | tf_op jit(solution)/shard_map/ppermute | solution.py:74
  130.7 80.3 %collective-permute-start.3 = (bf16[4,96,1152]{2,1,0:T(8,128)(2,1)}, bf16[4,96,1152]{2,1,0:T(8,128)(2,1)}, u32[]{:S(2)}, u32[]{:S(2)}) collective-permute-start(bf16[4,96,1152]{2,1,0:T(8,128)(2,1)} %get-tuple-element.37.refs_0_), channel_id=1, source_target_pairs={{0,2},{2,0},{4,6},{6,4},{8,10},{10,8},{12,14},{14,12},{1,3},{3,1},... | collective-permute-start | bytes 2654216 | tf_op jit(solution)/shard_map/ppermute | solution.py:74
  132.3 75.8 %collective-permute-start.7 = (bf16[4,96,1152]{2,1,0:T(8,128)(2,1)S(1)}, bf16[4,96,1152]{2,1,0:T(8,128)(2,1)}, u32[]{:S(2)}, u32[]{:S(2)}) collective-permute-start(bf16[4,96,1152]{2,1,0:T(8,128)(2,1)S(1)} %copy-done.31), channel_id=1, source_target_pairs={{0,8},{2,10},{4,12},{6,14},{8,0},{10,2},{12,4},{14,6},{1,9},{3,11}... | collective-permute-start | bytes 2654216 | tf_op jit(solution)/shard_map/ppermute | solution.py:74
  134.1 62.0 %copy-start.35 = (f32[1536]{0:T(1024)}, f32[1536]{0:T(1024)S(1)}, u32[]{:S(2)}) copy-start(f32[1536]{0:T(1024)S(1)} %convert_element_type.243) | copy-start | bytes 18436
  134.1 64.8 %copy-start.45 = (f32[512]{0:T(512)}, f32[512]{0:T(512)S(1)}, u32[]{:S(2)}) copy-start(f32[512]{0:T(512)S(1)} %convert_bitcast_fusion) | copy-start | bytes 6148
  147.7 104.4 %collective-permute-start.6 = (bf16[4,96,1152]{2,1,0:T(8,128)(2,1)S(1)}, bf16[4,96,1152]{2,1,0:T(8,128)(2,1)}, u32[]{:S(2)}, u32[]{:S(2)}) collective-permute-start(bf16[4,96,1152]{2,1,0:T(8,128)(2,1)S(1)} %copy-done.31), channel_id=1, source_target_pairs={{0,2},{2,0},{4,6},{6,4},{8,10},{10,8},{12,14},{14,12},{1,3},{3,1},... | collective-permute-start | bytes 2654216 | tf_op jit(solution)/shard_map/ppermute | solution.py:74
  151.0 41.7 %copy-start.2 = (bf16[4,128,1536]{2,1,0:T(8,128)(2,1)S(1)}, bf16[4,128,1536]{2,1,0:T(8,128)(2,1)}, u32[]{:S(2)}) copy-start(bf16[4,128,1536]{2,1,0:T(8,128)(2,1)} %refs_6_.1) | copy-start | bytes 4718596
  189.5 21.5 %collective-permute-start.5 = (bf16[4,96,1152]{2,1,0:T(8,128)(2,1)}, bf16[4,96,1152]{2,1,0:T(8,128)(2,1)}, u32[]{:S(2)}, u32[]{:S(2)}) collective-permute-start(bf16[4,96,1152]{2,1,0:T(8,128)(2,1)} %collective-permute-done.4.refs_2_), channel_id=1, source_target_pairs={{0,2},{2,0},{4,6},{6,4},{8,10},{10,8},{12,14},{14,12},{1,3},{3,1},... | collective-permute-start | bytes 2654216 | tf_op jit(solution)/shard_map/ppermute | solution.py:74
  197.5 47.8 %copy-start.47 = (bf16[1536]{0:T(1024)(128)(2,1)S(1)}, bf16[1536]{0:T(1024)(128)(2,1)}, u32[]{:S(2)}) copy-start(bf16[1536]{0:T(1024)(128)(2,1)} %param.20) | copy-start | bytes 9220
  198.8 45.1 %collective-permute-start.13 = (bf16[256,1536]{1,0:T(8,128)(2,1)S(1)}, bf16[256,1536]{1,0:T(8,128)(2,1)}, u32[]{:S(2)}, u32[]{:S(2)}) collective-permute-start(bf16[256,1536]{1,0:T(8,128)(2,1)S(1)} %constant_dynamic-slice_fusion.10), channel_id=1, source_target_pairs={{0,4},{2,6},{4,0},{6,2},{8,12},{10,14},{12,8},{14,10},{1,5},{3,7},... | collective-permute-start | bytes 2359304 | tf_op jit(solution)/shard_map/ppermute | solution.py:74
  208.1 44.2 %collective-permute-start.8 = (bf16[4,96,1152]{2,1,0:T(8,128)(2,1)}, bf16[4,96,1152]{2,1,0:T(8,128)(2,1)}, u32[]{:S(2)}, u32[]{:S(2)}) collective-permute-start(bf16[4,96,1152]{2,1,0:T(8,128)(2,1)} %collective-permute-done.7.refs_2_), channel_id=1, source_target_pairs={{0,2},{2,0},{4,6},{6,4},{8,10},{10,8},{12,14},{14,12},{1,3},{3,1},... | collective-permute-start | bytes 2654216 | tf_op jit(solution)/shard_map/ppermute | solution.py:74
  211.0 49.6 %collective-permute-start.21 = (bf16[256,1536]{1,0:T(8,128)(2,1)}, bf16[256,1536]{1,0:T(8,128)(2,1)}, u32[]{:S(2)}, u32[]{:S(2)}) collective-permute-start(bf16[256,1536]{1,0:T(8,128)(2,1)} %constant_dynamic-slice_fusion.9), channel_id=1, source_target_pairs={{0,4},{2,6},{4,0},{6,2},{8,12},{10,14},{12,8},{14,10},{1,5},{3,7},... | collective-permute-start | bytes 2359304 | tf_op jit(solution)/shard_map/ppermute | solution.py:74
  211.0 49.6 %collective-permute-start.10 = (bf16[4,96,1152]{2,1,0:T(8,128)(2,1)}, bf16[4,96,1152]{2,1,0:T(8,128)(2,1)}, u32[]{:S(2)}, u32[]{:S(2)}) collective-permute-start(bf16[4,96,1152]{2,1,0:T(8,128)(2,1)} %get-tuple-element.41.refs_0_), channel_id=1, source_target_pairs={{0,8},{2,10},{4,12},{6,14},{8,0},{10,2},{12,4},{14,6},{1,9},{3,11}... | collective-permute-start | bytes 2654216 | tf_op jit(solution)/shard_map/ppermute | solution.py:74
  243.9 19.7 %collective-permute-start.14 = (bf16[256,1536]{1,0:T(8,128)(2,1)}, bf16[256,1536]{1,0:T(8,128)(2,1)}, u32[]{:S(2)}, u32[]{:S(2)}) collective-permute-start(bf16[256,1536]{1,0:T(8,128)(2,1)} %collective-permute-done.13), channel_id=1, source_target_pairs={{0,1},{1,0},{2,3},{3,2},{4,5},{5,4},{6,7},{7,6},{8,9},{9,8},{10,11... | collective-permute-start | bytes 2359304 | tf_op jit(solution)/shard_map/ppermute | solution.py:74
  252.1 48.7 %collective-permute-start.19 = (bf16[512,1536]{1,0:T(8,128)(2,1)}, bf16[512,1536]{1,0:T(8,128)(2,1)}, u32[]{:S(2)}, u32[]{:S(2)}) collective-permute-start(bf16[512,1536]{1,0:T(8,128)(2,1)} %fusion.24), channel_id=1, source_target_pairs={{0,16},{16,0},{1,17},{17,1},{2,18},{18,2},{3,19},{19,3},{4,20},{20... | collective-permute-start | bytes 4718600 | tf_op jit(solution)/shard_map/ppermute | solution.py:74
  255.9 36.7 %collective-permute-start.9 = (bf16[4,96,1152]{2,1,0:T(8,128)(2,1)}, bf16[4,96,1152]{2,1,0:T(8,128)(2,1)}, u32[]{:S(2)}, u32[]{:S(2)}) collective-permute-start(bf16[4,96,1152]{2,1,0:T(8,128)(2,1)} %get-tuple-element.41.refs_0_), channel_id=1, source_target_pairs={{0,2},{2,0},{4,6},{6,4},{8,10},{10,8},{12,14},{14,12},{1,3},{3,1},... | collective-permute-start | bytes 2654216 | tf_op jit(solution)/shard_map/ppermute | solution.py:74
  260.6 23.6 %collective-permute-start.2 = (bf16[512,1536]{1,0:T(8,128)(2,1)}, bf16[512,1536]{1,0:T(8,128)(2,1)S(1)}, u32[]{:S(2)}, u32[]{:S(2)}) collective-permute-start(bf16[512,1536]{1,0:T(8,128)(2,1)} %multiply_convert_fusion.2), channel_id=1, source_target_pairs={{0,16},{16,0},{1,17},{17,1},{2,18},{18,2},{3,19},{19,3},{4,20},{20... | collective-permute-start | bytes 4718600 | tf_op jit(solution)/shard_map/ppermute | solution.py:74
  260.6 20.2 %collective-permute-start.22 = (bf16[256,1536]{1,0:T(8,128)(2,1)}, bf16[256,1536]{1,0:T(8,128)(2,1)S(1)}, u32[]{:S(2)}, u32[]{:S(2)}) collective-permute-start(bf16[256,1536]{1,0:T(8,128)(2,1)} %collective-permute-done.21), channel_id=1, source_target_pairs={{0,1},{1,0},{2,3},{3,2},{4,5},{5,4},{6,7},{7,6},{8,9},{9,8},{10,11... | collective-permute-start | bytes 2359304 | tf_op jit(solution)/shard_map/ppermute | solution.py:74
  263.5 33.7 %collective-permute-start.11 = (bf16[4,96,1152]{2,1,0:T(8,128)(2,1)}, bf16[4,96,1152]{2,1,0:T(8,128)(2,1)}, u32[]{:S(2)}, u32[]{:S(2)}) collective-permute-start(bf16[4,96,1152]{2,1,0:T(8,128)(2,1)} %collective-permute-done.10.refs_2_), channel_id=1, source_target_pairs={{0,2},{2,0},{4,6},{6,4},{8,10},{10,8},{12,14},{14,12},{1,3},{3,1},... | collective-permute-start | bytes 2654216 | tf_op jit(solution)/shard_map/ppermute | solution.py:74
  280.8 66.5 %collective-permute-start.15 = (bf16[512,1536]{1,0:T(8,128)(2,1)}, bf16[512,1536]{1,0:T(8,128)(2,1)}, u32[]{:S(2)}, u32[]{:S(2)}) collective-permute-start(bf16[512,1536]{1,0:T(8,128)(2,1)} %pad_maximum_fusion.7), channel_id=1, source_target_pairs={{0,16},{16,0},{1,17},{17,1},{2,18},{18,2},{3,19},{19,3},{4,20},{20... | collective-permute-start | bytes 4718600 | tf_op jit(solution)/shard_map/ppermute | solution.py:74
  284.2 53.6 %collective-permute-start.23 = (bf16[512,1536]{1,0:T(8,128)(2,1)}, bf16[512,1536]{1,0:T(8,128)(2,1)}, u32[]{:S(2)}, u32[]{:S(2)}) collective-permute-start(bf16[512,1536]{1,0:T(8,128)(2,1)} %pad_maximum_fusion.8), channel_id=1, source_target_pairs={{0,16},{16,0},{1,17},{17,1},{2,18},{18,2},{3,19},{19,3},{4,20},{20... | collective-permute-start | bytes 4718600 | tf_op jit(solution)/shard_map/ppermute | solution.py:74
  324.2 288.3 %collective-permute-start.12 = (bf16[512,1536]{1,0:T(8,128)(2,1)}, bf16[512,1536]{1,0:T(8,128)(2,1)}, u32[]{:S(2)}, u32[]{:S(2)}) collective-permute-start(bf16[512,1536]{1,0:T(8,128)(2,1)} %slice.216), channel_id=1, source_target_pairs={{0,16},{16,0},{1,17},{17,1},{2,18},{18,2},{3,19},{19,3},{4,20},{20... | collective-permute-start | bytes 4718600 | tf_op jit(solution)/shard_map/ppermute | solution.py:74
  337.8 98.1 %collective-permute-start.20 = (bf16[512,1536]{1,0:T(8,128)(2,1)}, bf16[512,1536]{1,0:T(8,128)(2,1)}, u32[]{:S(2)}, u32[]{:S(2)}) collective-permute-start(bf16[512,1536]{1,0:T(8,128)(2,1)} %slice.214), channel_id=1, source_target_pairs={{0,16},{16,0},{1,17},{17,1},{2,18},{18,2},{3,19},{19,3},{4,20},{20... | collective-permute-start | bytes 4718600 | tf_op jit(solution)/shard_map/ppermute | solution.py:74
  388.6 56.3 %collective-permute-start.30 = (bf16[2,2,2,96,1152]{4,3,2,0,1:T(8,128)(2,1)}, bf16[2,2,2,96,1152]{4,3,2,0,1:T(8,128)(2,1)}, u32[]{:S(2)}, u32[]{:S(2)}) collective-permute-start(bf16[2,2,2,96,1152]{4,3,2,0,1:T(8,128)(2,1)} %bitcast.147), channel_id=1, source_target_pairs={{0,2},{2,0},{4,6},{6,4},{8,10},{10,8},{12,14},{14,12},{1,3},{3,1},... | collective-permute-start | bytes 5308424 | tf_op jit(solution)/shard_map/ppermute | solution.py:74
  390.9 48.8 %collective-permute-start.16 = (bf16[512,1536]{1,0:T(8,128)(2,1)}, bf16[512,1536]{1,0:T(8,128)(2,1)}, u32[]{:S(2)}, u32[]{:S(2)}) collective-permute-start(bf16[512,1536]{1,0:T(8,128)(2,1)} %slice.215), channel_id=1, source_target_pairs={{0,16},{16,0},{1,17},{17,1},{2,18},{18,2},{3,19},{19,3},{4,20},{20... | collective-permute-start | bytes 4718600 | tf_op jit(solution)/shard_map/ppermute | solution.py:74
  399.7 43.0 %collective-permute-start.24 = (bf16[512,1536]{1,0:T(8,128)(2,1)S(1)}, bf16[512,1536]{1,0:T(8,128)(2,1)}, u32[]{:S(2)}, u32[]{:S(2)}) collective-permute-start(bf16[512,1536]{1,0:T(8,128)(2,1)S(1)} %slice.213), channel_id=1, source_target_pairs={{0,16},{16,0},{1,17},{17,1},{2,18},{18,2},{3,19},{19,3},{4,20},{20... | collective-permute-start | bytes 4718600 | tf_op jit(solution)/shard_map/ppermute | solution.py:74
  435.9 41.5 %collective-permute-start.32 = (bf16[2,2,2,96,1152]{4,3,2,0,1:T(8,128)(2,1)S(1)}, bf16[2,2,2,96,1152]{4,3,2,0,1:T(8,128)(2,1)S(1)}, u32[]{:S(2)}, u32[]{:S(2)}) collective-permute-start(bf16[2,2,2,96,1152]{4,3,2,0,1:T(8,128)(2,1)S(1)} %bitcast.182), channel_id=1, source_target_pairs={{0,2},{2,0},{4,6},{6,4},{8,10},{10,8},{12,14},{14,12},{1,3},{3,1},... | collective-permute-start | bytes 5308424 | tf_op jit(solution)/shard_map/ppermute | solution.py:74
  439.7 74.7 %collective-permute-start.34 = (bf16[2,2,2,96,1152]{4,3,2,0,1:T(8,128)(2,1)S(1)}, bf16[2,2,2,96,1152]{4,3,2,0,1:T(8,128)(2,1)S(1)}, u32[]{:S(2)}, u32[]{:S(2)}) collective-permute-start(bf16[2,2,2,96,1152]{4,3,2,0,1:T(8,128)(2,1)S(1)} %bitcast.181), channel_id=1, source_target_pairs={{0,2},{2,0},{4,6},{6,4},{8,10},{10,8},{12,14},{14,12},{1,3},{3,1},... | collective-permute-start | bytes 5308424 | tf_op jit(solution)/shard_map/ppermute | solution.py:74
  442.7 169.8 %collective-permute-start.17 = (bf16[512,1536]{1,0:T(8,128)(2,1)S(1)}, bf16[512,1536]{1,0:T(8,128)(2,1)S(1)}, u32[]{:S(2)}, u32[]{:S(2)}) collective-permute-start(bf16[512,1536]{1,0:T(8,128)(2,1)S(1)} %fusion.19), channel_id=1, source_target_pairs={{0,4},{2,6},{4,0},{6,2},{8,12},{10,14},{12,8},{14,10},{1,5},{3,7},... | collective-permute-start | bytes 4718600 | tf_op jit(solution)/shard_map/ppermute | solution.py:74
  444.9 71.0 %collective-permute-start.25 = (bf16[256,1536]{1,0:T(8,128)(2,1)S(1)}, bf16[256,1536]{1,0:T(8,128)(2,1)S(1)}, u32[]{:S(2)}, u32[]{:S(2)}) collective-permute-start(bf16[256,1536]{1,0:T(8,128)(2,1)S(1)} %get-tuple-element.78), channel_id=1, source_target_pairs={{0,4},{2,6},{4,0},{6,2},{8,12},{10,14},{12,8},{14,10},{1,5},{3,7},... | collective-permute-start | bytes 2359304 | tf_op jit(solution)/shard_map/ppermute | solution.py:74
  477.5 41.4 %collective-permute-start.27 = (bf16[256,1536]{1,0:T(8,128)(2,1)S(1)}, bf16[256,1536]{1,0:T(8,128)(2,1)S(1)}, u32[]{:S(2)}, u32[]{:S(2)}) collective-permute-start(bf16[256,1536]{1,0:T(8,128)(2,1)S(1)} %get-tuple-element.79), channel_id=1, source_target_pairs={{0,4},{2,6},{4,0},{6,2},{8,12},{10,14},{12,8},{14,10},{1,5},{3,7},... | collective-permute-start | bytes 2359304 | tf_op jit(solution)/shard_map/ppermute | solution.py:74
  514.4 77.4 %collective-permute-start.31 = (bf16[2,2,96,1152]{3,2,1,0:T(8,128)(2,1)S(1)}, bf16[2,2,96,1152]{3,2,1,0:T(8,128)(2,1)S(1)}, u32[]{:S(2)}, u32[]{:S(2)}) collective-permute-start(bf16[2,2,96,1152]{3,2,1,0:T(8,128)(2,1)S(1)} %fusion.44), channel_id=1, source_target_pairs={{0,8},{2,10},{4,12},{6,14},{8,0},{10,2},{12,4},{14,6},{1,9},{3,11}... | collective-permute-start | bytes 2654216 | tf_op jit(solution)/shard_map/ppermute | solution.py:74
  514.4 98.0 %slice-start.4 = ((s8[6291456]{0:T(1024)(128)(4,1)}), s8[4194304]{0:T(1024)(128)(4,1)S(1)}, s32[]{:S(2)}) async-start(s8[6291456]{0:T(1024)(128)(4,1)} %bitcast.170), calls=%async_computation.4 | async-start | bytes 8388608
  515.9 96.5 %slice-start.5 = ((s8[6291456]{0:T(1024)(128)(4,1)}), s8[2097152]{0:T(1024)(128)(4,1)S(1)}, s32[]{:S(2)}) async-start(s8[6291456]{0:T(1024)(128)(4,1)} %bitcast.170), calls=%async_computation.5 | async-start | bytes 4194304
  515.9 94.9 %collective-permute-start.33 = (bf16[2,2,96,1152]{3,2,1,0:T(8,128)(2,1)S(1)}, bf16[2,2,96,1152]{3,2,1,0:T(8,128)(2,1)S(1)}, u32[]{:S(2)}, u32[]{:S(2)}) collective-permute-start(bf16[2,2,96,1152]{3,2,1,0:T(8,128)(2,1)S(1)} %fusion.45), channel_id=1, source_target_pairs={{0,8},{2,10},{4,12},{6,14},{8,0},{10,2},{12,4},{14,6},{1,9},{3,11}... | collective-permute-start | bytes 2654216 | tf_op jit(solution)/shard_map/ppermute | solution.py:74
  518.9 216.1 %collective-permute-start.35 = (bf16[2,2,96,1152]{3,2,1,0:T(8,128)(2,1)}, bf16[2,2,96,1152]{3,2,1,0:T(8,128)(2,1)}, u32[]{:S(2)}, u32[]{:S(2)}) collective-permute-start(bf16[2,2,96,1152]{3,2,1,0:T(8,128)(2,1)} %fusion.46), channel_id=1, source_target_pairs={{0,8},{2,10},{4,12},{6,14},{8,0},{10,2},{12,4},{14,6},{1,9},{3,11}... | collective-permute-start | bytes 2654216 | tf_op jit(solution)/shard_map/ppermute | solution.py:74
  591.9 24.4 %collective-permute-start.26 = (bf16[256,1536]{1,0:T(8,128)(2,1)S(1)}, bf16[256,1536]{1,0:T(8,128)(2,1)S(1)}, u32[]{:S(2)}, u32[]{:S(2)}) collective-permute-start(bf16[256,1536]{1,0:T(8,128)(2,1)S(1)} %get-tuple-element.72), channel_id=1, source_target_pairs={{0,1},{1,0},{2,3},{3,2},{4,5},{5,4},{6,7},{7,6},{8,9},{9,8},{10,11... | collective-permute-start | bytes 2359304 | tf_op jit(solution)/shard_map/ppermute | solution.py:74
  610.8 20.4 %collective-permute-start.28 = (bf16[256,1536]{1,0:T(8,128)(2,1)S(1)}, bf16[256,1536]{1,0:T(8,128)(2,1)S(1)}, u32[]{:S(2)}, u32[]{:S(2)}) collective-permute-start(bf16[256,1536]{1,0:T(8,128)(2,1)S(1)} %get-tuple-element.73), channel_id=1, source_target_pairs={{0,1},{1,0},{2,3},{3,2},{4,5},{5,4},{6,7},{7,6},{8,9},{9,8},{10,11... | collective-permute-start | bytes 2359304 | tf_op jit(solution)/shard_map/ppermute | solution.py:74
  614.7 49.2 %collective-permute-start.18 = (bf16[512,1536]{1,0:T(8,128)(2,1)S(1)}, bf16[512,1536]{1,0:T(8,128)(2,1)S(1)}, u32[]{:S(2)}, u32[]{:S(2)}) collective-permute-start(bf16[512,1536]{1,0:T(8,128)(2,1)S(1)} %fusion.22), channel_id=1, source_target_pairs={{0,1},{1,0},{2,3},{3,2},{4,5},{5,4},{6,7},{7,6},{8,9},{9,8},{10,11... | collective-permute-start | bytes 4718600 | tf_op jit(solution)/shard_map/ppermute | solution.py:74
  690.3 39.7 %copy-start.3 = (bf16[4,128,1536]{2,1,0:T(8,128)(2,1)S(1)}, bf16[4,128,1536]{2,1,0:T(8,128)(2,1)}, u32[]{:S(2)}) copy-start(bf16[4,128,1536]{2,1,0:T(8,128)(2,1)} %refs_6_.1) | copy-start | bytes 4718596
  734.3 87.9 %collective-permute-start.29 = (bf16[512,1536]{1,0:T(8,128)(2,1)S(1)}, bf16[512,1536]{1,0:T(8,128)(2,1)}, u32[]{:S(2)}, u32[]{:S(2)}) collective-permute-start(bf16[512,1536]{1,0:T(8,128)(2,1)S(1)} %get-tuple-element.69), channel_id=1, source_target_pairs={{0,1},{1,0},{2,3},{3,2},{4,5},{5,4},{6,7},{7,6},{8,9},{9,8},{10,11... | collective-permute-start | bytes 4718600 | tf_op jit(solution)/shard_map/ppermute | solution.py:74
  744.8 77.4 %copy-start.37 = (f32[1536]{0:T(1024)S(1)}, f32[1536]{0:T(1024)}, u32[]{:S(2)}) copy-start(f32[1536]{0:T(1024)} %convert_element_type.238) | copy-start | bytes 18436
  (68 other events, 681.5 us)
where the time goes:
time: 840 us; the launch traced here: 833 us
  waiting for transfers between devices  315 us (38%)
  Pallas kernels  249 us (30%)
  matrix products  151 us (18%)
  other arithmetic  50.2 us (6%)
  local copies, waits for them, and re-layouts  36.9 us (4%)
  starting transfers between devices  28.3 us (3%)
    ppermute x36, waiting for transfers between devices, flip(): return lax.ppermute(values, axis, [(i, i ^ mask) for i in range(size)])  315 us
    pallas_call x2, Pallas kernels, reduce_pieces(): pl.pallas_call(functools.partial(reduce_kernel, places, flags, int(vector...  107 us
    pallas_call x2, Pallas kernels, gather_pieces(): pl.pallas_call(functools.partial(gather_kernel, places, flags, extra, blo...  96.1 us
    dot_general x8, matrix products, grad_of_weight(): lax.dot_general(left, right, (((0,), (0,)), ((), ())), preferred_element_...  59.7 us
    dot_general x8, matrix products, plain_dot(): return jnp.dot(left, right, preferred_element_type=F32)  55.1 us
    dot_general x8, matrix products, through_weight(): lax.dot_general(left, right, (((1,), (1,)), ((), ())), preferred_element_...  36 us
    ppermute x36, starting transfers between devices, flip(): return lax.ppermute(values, axis, [(i, i ^ mask) for i in range(size)])  28.3 us
    pallas_call x1, Pallas kernels, attend_back(): pl.pallas_call(functools.partial(attend_back_kernel, heads, head_size, fa...  21.1 us
  transfers between devices with their start and end apart: 36, of which 14 were waited for; matrix products, arithmetic and copies ran while one was open for 26% of the time, Pallas kernels for 23%

commit v1 on v0

--- a/solution.py
+++ b/solution.py
@@ -625,9 +625,114 @@
     return out.reshape(total * rows, columns)
 
 
-def sum_heads(part):
-    low = lax.reduce_precision(part, 8, 7).astype(BF16)
-    return low.astype(F32) + flip(low, "head", 1).astype(F32)
+def unit_chunk(block):
+    third = block // 3
+    return third if block % 3 == 0 and third % LANES == 0 else LANES
+
+
+def ffn_forward_kernel(rows_ref, live_ref, gate_ref, up_ref, g_ref, u_ref, z_ref):
+    block = gate_ref.shape[1]
+    chunk = unit_chunk(block)
+
+    def step(j, carry):
+        part = pl.ds(pl.multiple_of(j * chunk, LANES), chunk)
+        live = live_ref[:, part] > 0.0
+        gate_pre = jnp.where(live, plain_dot(rows_ref[...], gate_ref[:, part]), 0.0)
+        up_pre = jnp.where(live, plain_dot(rows_ref[...], up_ref[:, part]), 0.0)
+        g_ref[:, part] = gate_pre
+        u_ref[:, part] = up_pre
+        z_ref[:, part] = (gate_pre * jax.nn.sigmoid(gate_pre) * up_pre).astype(BF16)
+        return carry
+
+    lax.fori_loop(0, block // chunk, step, 0)
+
+
+def ffn_back_kernel(cot_ref, g_ref, u_ref, gate_ref, up_ref, down_ref, dg_ref, du_ref, e_ref):
+    width, block = gate_ref.shape
+    chunk = unit_chunk(block)
+
+    def step(j, carry):
+        part = pl.ds(pl.multiple_of(j * chunk, LANES), chunk)
+        d_product = plain_dot(cot_ref[...], down_ref[:, part]).astype(BF16).astype(F32)
+        gate_pre = g_ref[:, part]
+        sigmoid_gate = jax.nn.sigmoid(gate_pre)
+        slope = sigmoid_gate * (1.0 + gate_pre * (1.0 - sigmoid_gate))
+        dg_ref[:, part] = (d_product * u_ref[:, part] * slope).astype(BF16)
+        du_ref[:, part] = (d_product * (gate_pre * sigmoid_gate)).astype(BF16)
+        return carry
+
+    lax.fori_loop(0, block // chunk, step, 0)
+    wide_chunk = unit_chunk(width)
+
+    def fold(j, carry):
+        part = pl.ds(pl.multiple_of(j * wide_chunk, LANES), wide_chunk)
+        e_ref[:, part] = (
+            dot_nt(dg_ref[...], gate_ref[part, :]) + dot_nt(du_ref[...], up_ref[part, :])
+        ).astype(BF16)
+        return carry
+
+    lax.fori_loop(0, width // wide_chunk, fold, 0)
+
+
+def tile_spec(tile, width):
+    return pl.BlockSpec((tile, width), lambda i: (i, 0))
+
+
+def whole_spec(array):
+    return pl.BlockSpec(array.shape, lambda i: (0, 0), pipeline_mode=pl.Buffered(1))
+
+
+def ffn_forward(rows, live, gate, up):
+    count, width = rows.shape
+    block = gate.shape[1]
+    tile = count // 4
+    return pl.pallas_call(
+        ffn_forward_kernel,
+        grid=(4,),
+        out_shape=(
+            jax.ShapeDtypeStruct((count, block), F32),
+            jax.ShapeDtypeStruct((count, block), F32),
+            jax.ShapeDtypeStruct((count, block), BF16),
+        ),
+        in_specs=[tile_spec(tile, width), whole_spec(live), whole_spec(gate), whole_spec(up)],
+        out_specs=(tile_spec(tile, block),) * 3,
+        cost_estimate=pl.CostEstimate(
+            flops=4 * count * width * block,
+            bytes_accessed=10 * count * block + 4 * width * block,
+            transcendentals=count * block,
+        ),
+        name="ffn_forward",
+    )(rows, live, gate, up)
+
+
+def ffn_back(cots, gate_pre, up_pre, gate, up, down):
+    count, width = cots.shape
+    block = gate.shape[1]
+    tile = count // 4
+    return pl.pallas_call(
+        ffn_back_kernel,
+        grid=(4,),
+        out_shape=(
+            jax.ShapeDtypeStruct((count, block), BF16),
+            jax.ShapeDtypeStruct((count, block), BF16),
+            jax.ShapeDtypeStruct((count, width), BF16),
+        ),
+        in_specs=[
+            tile_spec(tile, width),
+            tile_spec(tile, block),
+            tile_spec(tile, block),
+            whole_spec(gate),
+            whole_spec(up),
+            whole_spec(down),
+        ],
+        out_specs=(tile_spec(tile, block), tile_spec(tile, block), tile_spec(tile, width)),
+        cost_estimate=pl.CostEstimate(
+            flops=6 * count * width * block,
+            bytes_accessed=12 * count * block + 6 * width * block,
+            transcendentals=count * block,
+        ),
+        name="ffn_back",
+    )(cots, gate_pre, up_pre, gate, up, down)
 
 
 def in_order(own, other, head, axis):
@@ -637,30 +742,26 @@
     )
 
 
-def both_cores(values):
-    return jnp.concatenate([values, flip(values, "dp", 1)], axis=0)
-
-
 def far_rows(values, head):
     half = values.shape[0] // 2
     got = flip(lax.dynamic_slice_in_dim(values, head * half, half, 0), "seq", 2)
-    return in_order(got, flip(got, "head", 1), head, 0)
-
-
-def core_sum(part):
-    half = part.shape[0] // 2
-    return part[:half] + flip(part[half:].astype(BF16), "dp", 1).astype(F32)
-
-
-def collect(near, far, pieces):
-    far_low = core_sum(far).astype(BF16)
-    near = core_sum(near)
-    size = near.shape[0] // pieces
-    out = []
-    for i in range(pieces):
-        rows = slice(i * size, (i + 1) * size)
-        out.append(sum_heads(near[rows] + flip(far_low[rows], "seq", 2).astype(F32)))
-    return jnp.concatenate(out, axis=0) if pieces > 1 else out[0]
+    other = flip(got, "head", 1)
+    return in_order(got, other, head, 0)
+
+
+def four_rows(own, far):
+    blocks = [own, flip(own, "dp", 1), far, flip(far, "dp", 1)]
+    return lax.optimization_barrier(jnp.concatenate(blocks, axis=0))
+
+
+def core_sums(part):
+    blocks = part.reshape(4, -1, part.shape[-1])
+    far = flip(blocks[3].astype(BF16), "dp", 1)
+    near = flip(blocks[1].astype(BF16), "dp", 1)
+    return (
+        blocks[0].astype(F32) + near.astype(F32),
+        blocks[2].astype(F32) + far.astype(F32),
+    )
 
 
 def on_device(
@@ -748,12 +849,17 @@
     local_kv = local_kv.reshape(row_count, row_width, 2 * head_size)
     (all_kv,) = gather_pieces([local_kv], (0,), 1)
 
-    up_parts = column_gather(after(near_up, all_kv))
+    up_parts = column_gather(near_up)
     full_gate = side_gather(gate_parts)
     full_up = side_gather(up_parts)
 
     out_other = flip(full_out, "head", 1)
     out_all = in_order(full_out, out_other, head, 1)
+
+    live_rows = (segment_ids != 0).astype(F32).reshape(tokens, 1)
+    cotangent = out_cot.reshape(tokens, model_width).astype(F32) * live_rows
+    cot_own = cotangent.astype(BF16)
+    cot_far = far_rows(cot_own, head)
 
     mixed = attend(queries, all_kv, marks, heads, head_size, factor).reshape(tokens, wide)
     mixed_all = in_order(mixed, flip(mixed, "head", 1), head, 1)
@@ -763,55 +869,41 @@
     normed_own = (middle * scale_two * gain_two).astype(BF16)
     normed_far = far_rows(normed_own, head)
 
-    down_parts = column_gather(after(near_down, normed_own))
+    down_parts = column_gather(near_down)
     full_down = side_gather(down_parts)
-
-    live_rows = (segment_ids != 0).astype(F32).reshape(tokens, 1)
-    cotangent = out_cot.reshape(tokens, model_width).astype(F32) * live_rows
-    cot_own = cotangent.astype(BF16)
-    cot_far = far_rows(after(cot_own, normed_own), head)
 
     drawn_back = 4 * block - units
     live_units = (jnp.arange(block) >= drawn_back) | (level * 2 + core < 3)
-    forward, backward, norms, cots = [], [], [], []
-    for own_rows, own_cot in ((normed_own, cot_own), (normed_far, cot_far)):
-        rows = both_cores(own_rows)
-        gate_pre = jnp.where(live_units, plain_dot(rows, full_gate), 0.0)
-        up_pre = jnp.where(live_units, plain_dot(rows, full_up), 0.0)
-        sigmoid_gate = jax.nn.sigmoid(gate_pre)
-        activated = gate_pre * sigmoid_gate
-        product = (activated * up_pre).astype(BF16)
-        cot_rows = both_cores(own_cot)
-        d_product = plain_dot(cot_rows, full_down).astype(BF16).astype(F32)
-        slope = sigmoid_gate * (1.0 + gate_pre * (1.0 - sigmoid_gate))
-        d_gate = (d_product * up_pre * slope).astype(BF16)
-        d_up = (d_product * activated).astype(BF16)
-        norms.append(rows)
-        cots.append(cot_rows)
-        forward.append(product)
-        backward.append((d_gate, d_up))
-    back_parts = [
-        through_weight(d_gate, full_gate) + through_weight(d_up, full_up)
-        for d_gate, d_up in backward
-    ]
-    back_two = collect(*back_parts, 2)
-
-    def weight_grad(lefts, rights):
-        return (
-            grad_of_weight(lefts[0], rights[0]) + grad_of_weight(lefts[1], rights[1])
-        ).astype(BF16)
-
-    grad_down = weight_grad(cots, forward)
-    grad_gate = weight_grad(norms, [pair[0] for pair in backward])
-    grad_up = weight_grad(norms, [pair[1] for pair in backward])
-    result = middle + collect(*[through_weight(part, full_down) for part in forward], 1)
-    layer_out = result.astype(BF16).reshape(row_count, row_width, model_width)
+    norms = four_rows(normed_own, normed_far)
+    cots = four_rows(cot_own, cot_far)
+    gate_pre, up_pre, product = ffn_forward(
+        norms, live_units.astype(F32)[None], full_gate, full_up
+    )
+    grad_down = grad_of_weight(cots, product).astype(BF16)
+    d_gate, d_up, back_all = ffn_back(
+        cots, gate_pre, up_pre, full_gate, full_up, full_down
+    )
+
+    near, far = core_sums(back_all)
+    far_low = far.astype(BF16)
+    halves, crossed = [], []
+    for i in range(2):
+        rows = slice(i * tokens // 2, (i + 1) * tokens // 2)
+        crossed.append(flip(far_low[rows], "seq", 2))
+        part = near[rows] + crossed[i].astype(F32)
+        low = lax.reduce_precision(part, 8, 7).astype(BF16)
+        other = flip(low, "head", 1)
+        halves.append(low.astype(F32) + other.astype(F32))
+    back_two = jnp.concatenate(halves, axis=0)
+
+    grad_gate = grad_of_weight(norms, d_gate).astype(BF16)
+    grad_up = grad_of_weight(norms, d_up).astype(BF16)
 
     ffn_sums = []
     for grad in (grad_down, grad_gate, grad_up):
         blocks = grad.reshape(2, columns, 2, 2, shard, block)
-        half = take(blocks, side, 3).astype(F32)
-        half = half + flip(take(blocks, 1 - side, 3), "seq", 1).astype(F32)
+        got = flip(take(blocks, 1 - side, 3), "seq", 1)
+        half = take(blocks, side, 3).astype(F32) + got.astype(F32)
         low = half.astype(BF16)
         total = take(half, column, 1)
         for k in range(1, columns):
@@ -822,6 +914,21 @@
     d_middle = cotangent + norm_back(back_two, middle, scale_two, gain_two)
     d_middle_low = d_middle.astype(BF16)
     d_mixed = plain_dot(d_middle_low, full_out).astype(BF16)
+
+    result_all = through_weight(product, full_down).astype(BF16)
+    near, far = core_sums(result_all)
+    half = tokens // 2
+    mine = [lax.dynamic_slice_in_dim(part, head * half, half, 0) for part in (near, far)]
+    theirs = [
+        lax.dynamic_slice_in_dim(part, (1 - head) * half, half, 0) for part in (near, far)
+    ]
+    got = flip(jnp.concatenate(theirs, axis=0).astype(BF16), "head", 1).astype(F32)
+    got_far = flip((mine[1] + got[half:]).astype(BF16), "seq", 2).astype(F32)
+    total = mine[0] + got[:half] + got_far
+    out_half = (lax.dynamic_slice_in_dim(middle, head * half, half, 0) + total).astype(BF16)
+    out_other = flip(out_half, "head", 1)
+    layer_out = in_order(out_half, out_other, head, 0)
+    layer_out = layer_out.reshape(row_count, row_width, model_width)
 
     turns = (
         jnp.concatenate([cosine, cosine], axis=1).reshape(row_count, row_width, head_size),

time: 840 us -> 809 us (0.963)
  matrix products: 151 us -> 65.3 us
  Pallas kernels: 249 us -> 324 us
  waiting for transfers between devices: 315 us -> 275 us
  local copies, waits for them, and re-layouts: 36.9 us -> 50.1 us
    pallas_call x0 -> x2, Pallas kernels: none -> 69.2 us  [the longest x1 41.1 us: ffn_back(): pl.pallas_call(ffn_back_kernel, grid=(4,), out_shape=(jax.ShapeDtypeStruc...]
    dot_general x8 -> x2, matrix products: 55.1 us -> 6.47 us  [plain_dot(): return jnp.dot(left, right, preferred_element_type=F32)]
    ppermute x36 -> x37, waiting for transfers between devices: 315 us -> 275 us  [flip(): return lax.ppermute(values, axis, [(i, i ^ mask) for i in range(size)])]
    dot_general x8 -> x3, matrix products: 36 us -> 16 us  [through_weight(): lax.dot_general(left, right, (((1,), (1,)), ((), ())), preferred_element_...]
    dot_general x8 -> x5, matrix products: 59.7 us -> 42.8 us  [grad_of_weight(): lax.dot_general(left, right, (((0,), (0,)), ((), ())), preferred_element_...]
    ppermute x36 -> x37, starting transfers between devices: 28.3 us -> 32.4 us  [flip(): return lax.ppermute(values, axis, [(i, i ^ mask) for i in range(size)])]
  transfers between devices with their start and end apart: 36 -> 37, of which waited for: 14 -> 14; matrix products, arithmetic and copies ran while one was open for 26% -> 15% of each run, Pallas kernels for 23% -> 24%
where the time goes in v1:
time: 809 us; the launch traced here: 804 us
  Pallas kernels  324 us (40%)
  waiting for transfers between devices  275 us (34%)
  matrix products  65.3 us (8%)
  other arithmetic  55.3 us (7%)
  local copies, waits for them, and re-layouts  50.1 us (6%)
  starting transfers between devices  32.4 us (4%)
    ppermute x37, waiting for transfers between devices, flip(): return lax.ppermute(values, axis, [(i, i ^ mask) for i in range(size)])  275 us
    pallas_call x2, Pallas kernels, reduce_pieces(): pl.pallas_call(functools.partial(reduce_kernel, places, flags, int(vector...  113 us
    pallas_call x2, Pallas kernels, gather_pieces(): pl.pallas_call(functools.partial(gather_kernel, places, flags, extra, blo...  96.1 us
    dot_general x5, matrix products, grad_of_weight(): lax.dot_general(left, right, (((0,), (0,)), ((), ())), preferred_element_...  42.8 us
    pallas_call x1, Pallas kernels, ffn_back(): pl.pallas_call(ffn_back_kernel, grid=(4,), out_shape=(jax.ShapeDtypeStruc...  41.1 us
    ppermute x37, starting transfers between devices, flip(): return lax.ppermute(values, axis, [(i, i ^ mask) for i in range(size)])  32.4 us
    pallas_call x1, Pallas kernels, ffn_forward(): pl.pallas_call(ffn_forward_kernel, grid=(4,), out_shape=(jax.ShapeDtypeSt...  28.1 us
    pallas_call x1, Pallas kernels, attend_back(): pl.pallas_call(functools.partial(attend_back_kernel, heads, head_size, fa...  21.1 us
  transfers between devices with their start and end apart: 37, of which 14 were waited for; matrix products, arithmetic and copies ran while one was open for 15% of the time, Pallas kernels for 24%

profile of v1, /device:TPU:0, one launch (start us, length us, event | category | flops | bytes accessed | tf_op | source)
XLA Modules:
  0.0 803.8 jit_solution(4304790023991972845)
XLA Ops:
  4.9 61.0 %shard_map.263 = (bf16[16,96,1024]{2,1,0:T(8,128)(2,1)}, bf16[16,96,768]{2,1,0:T(8,128)(2,1)}, s32[8,8,128]{2,1,0:T(8,128)}, bf16[4,96,1152]{2,1,0:T(8,128)(2,1)...) custom-call(bf16[96,1024]{1,0:T(8,128)(2,1)} %pad_maximum_fusion.10.refs_0_, ...), custom_call_target="tpu_custom_call" | custom-call | bytes 100000000 | tf_op jit(solution)/shard_map/pallas_call | solution.py:361
  67.6 4.2 convolution_add_fusion
  76.6 35.1 %shard_map.264.kv_ref = bf16[8,4,128,256]{3,2,1,0:T(8,128)(2,1)} custom-call(bf16[4,128,256]{2,1,0:T(8,128)(2,1)} %bitcast.156), custom_call_target="tpu_custom_call" | custom-call | bytes 100000000 | tf_op jit(solution)/shard_map/pallas_call | solution.py:361
  113.5 13.9 %attend.1 = bf16[4,128,768]{2,1,0:T(8,128)(2,1)} custom-call(bf16[4,128,768]{2,1,0:T(8,128)(2,1)} %copy.56.q_ref, bf16[8,4,128,256]{3,2,1,0:T(8,128)(2,1)} %shard_map.264.kv_ref, s32[4,128,1]{2,1,0:T(8,128)} %copy.57.sq_ref, s32[4,128,1]{2,1,0:T(8,128)} %copy.58.pq_ref, s32[4,1,1024]{2,1,0:T(1,128)} %bitcast.171, s32[4,1,1024]{2,1,0:T(1,128)} %bitcast.169), custom_call_target="tpu_custom_call" | custom-call | flops 1610612736 | bytes 3670016 | tf_op jit(solution)/shard_map/attend/pallas_call | solution.py:161
  134.3 11.8 %collective-permute-done = bf16[512,768]{1,0:T(8,128)(2,1)} collective-permute-done((bf16[512,768]{1,0:T(8,128)(2,1)}, bf16[512,768]{1,0:T(8,128)(2,1)}, u32[]{:S(2)}, u32[]{:S(2)}) %collective-permute-start) | collective-permute-done | bytes 786464 | tf_op jit(solution)/shard_map/ppermute | solution.py:74
  146.1 18.8 %collective-permute-done.21 = bf16[256,1536]{1,0:T(8,128)(2,1)} collective-permute-done((bf16[256,1536]{1,0:T(8,128)(2,1)S(1)}, bf16[256,1536]{1,0:T(8,128)(2,1)}, u32[]{:S(2)}, u32[]{:S(2)}) %collective-permute-start.21) | collective-permute-done | bytes 786464 | tf_op jit(solution)/shard_map/ppermute | solution.py:74
  170.0 2.7 multiply_reduce_fusion.2
  175.2 7.5 collective-permute-done.22
  182.7 2.2 constant_dynamic-update-slice_fusion.7
  185.0 19.2 %collective-permute-done.3 = bf16[256,1536]{1,0:T(8,128)(2,1)S(1)} collective-permute-done((bf16[256,1536]{1,0:T(8,128)(2,1)S(1)}, bf16[256,1536]{1,0:T(8,128)(2,1)S(1)}, u32[]{:S(2)}, u32[]{:S(2)}) %collective-permute-start.3) | collective-permute-done | bytes 786464 | tf_op jit(solution)/shard_map/ppermute | solution.py:74
  206.7 2.8 collective-permute-start.13
  209.5 13.9 %collective-permute-done.4 = bf16[256,1536]{1,0:T(8,128)(2,1)S(1)} collective-permute-done((bf16[256,1536]{1,0:T(8,128)(2,1)S(1)}, bf16[256,1536]{1,0:T(8,128)(2,1)S(1)}, u32[]{:S(2)}, u32[]{:S(2)}) %collective-permute-start.4) | collective-permute-done | bytes 786464 | tf_op jit(solution)/shard_map/ppermute | solution.py:74
  226.9 17.5 %collective-permute-done.10.refs_2_ = bf16[4,96,1152]{2,1,0:T(8,128)(2,1)} collective-permute-done((bf16[4,96,1152]{2,1,0:T(8,128)(2,1)}, bf16[4,96,1152]{2,1,0:T(8,128)(2,1)}, u32[]{:S(2)}, u32[]{:S(2)}) %collective-permute-start.10) | collective-permute-done | bytes 884768 | tf_op jit(solution)/shard_map/ppermute | solution.py:74
  246.4 3.2 collective-permute-start.11
  249.7 10.1 %collective-permute-done.13.refs_2_ = bf16[4,96,1152]{2,1,0:T(8,128)(2,1)} collective-permute-done((bf16[4,96,1152]{2,1,0:T(8,128)(2,1)}, bf16[4,96,1152]{2,1,0:T(8,128)(2,1)}, u32[]{:S(2)}, u32[]{:S(2)}) %collective-permute-start.13) | collective-permute-done | bytes 884768 | tf_op jit(solution)/shard_map/ppermute | solution.py:74
  259.8 3.9 collective-permute-start.12
  267.8 3.6 join.3
  271.5 3.6 join.4
  275.1 14.4 %collective-permute-done.12.refs_1_ = bf16[4,96,1152]{2,1,0:T(8,128)(2,1)} collective-permute-done((bf16[4,96,1152]{2,1,0:T(8,128)(2,1)}, bf16[4,96,1152]{2,1,0:T(8,128)(2,1)}, u32[]{:S(2)}, u32[]{:S(2)}) %collective-permute-start.12) | collective-permute-done | bytes 884768 | tf_op jit(solution)/shard_map/ppermute | solution.py:74
  289.4 18.8 %collective-permute-done.14.refs_3_ = bf16[4,96,1152]{2,1,0:T(8,128)(2,1)} collective-permute-done((bf16[4,96,1152]{2,1,0:T(8,128)(2,1)}, bf16[4,96,1152]{2,1,0:T(8,128)(2,1)}, u32[]{:S(2)}, u32[]{:S(2)}) %collective-permute-start.14) | collective-permute-done | bytes 884768 | tf_op jit(solution)/shard_map/ppermute | solution.py:74
  308.2 3.6 join.5
  311.9 2.7 constant_dynamic-update-slice_fusion.5.cot_ref
  314.5 2.7 constant_dynamic-update-slice_fusion.rows_ref
  317.3 28.1 %ffn_forward.1 = (f32[2048,1152]{1,0:T(8,128)}, f32[2048,1152]{1,0:T(8,128)}, bf16[2048,1152]{1,0:T(8,128)(2,1)}) custom-call(bf16[2048,1536]{1,0:T(8,128)(2,1)} %constant_dynamic-update-slice_fusion.rows_ref, f32[1,1152]{1,0:T(1,128)} %or_convert_fusion.live_ref, bf16[1536,1152]{1,0:T(8,128)(2,1)} %bitcast.142, bf16[1536,1152]{1,0:T(8,128)(2,1)} %bitcast.144), custom_call_target="tpu_custom_call" | custom-call | flops 14495514624 | bytes 30670848 | tf_op jit(solution)/shard_map/ffn_forward/pallas_call | solution.py:689
  345.4 41.1 %ffn_back.1 = (bf16[2048,1152]{1,0:T(8,128)(2,1)}, bf16[2048,1152]{1,0:T(8,128)(2,1)}, bf16[2048,1536]{1,0:T(8,128)(2,1)}) custom-call(bf16[2048,1536]{1,0:T(8,128)(2,1)} %constant_dynamic-update-slice_fusion.5.cot_ref, f32[2048,1152]{1,0:T(8,128)} %get-tuple-element.44.g_ref, f32[2048,1152]{1,0:T(8,128)} %get-tuple-element.45.u_ref, ...), custom_call_target="tpu_custom_call" | custom-call | flops 21743271936 | bytes 38928384 | tf_op jit(solution)/shard_map/ffn_back/pallas_call | solution.py:712
  386.5 12.1 %convolution_convert_fusion.1 = bf16[1536,1152]{1,0:T(8,128)(2,1)S(1)} fusion(bf16[2048,1536]{1,0:T(8,128)(2,1)} %constant_dynamic-update-slice_fusion.rows_ref, bf16[2048,1152]{1,0:T(8,128)(2,1)} %get-tuple-element.50), kind=kOutput, calls=%fused_computation.1 | convolution fusion | flops 7249526784 | bytes 14548992 | tf_op jit(solution)/shard_map/dot_general | solution.py:55
  398.6 10.5 %convolution_convert_fusion = bf16[1536,1152]{1,0:T(8,128)(2,1)} fusion(bf16[2048,1536]{1,0:T(8,128)(2,1)S(1)} %copy-done.21, bf16[2048,1152]{1,0:T(8,128)(2,1)S(1)} %copy-done.45), kind=kOutput, calls=%fused_computation | convolution fusion | flops 7249526784 | bytes 14548992 | tf_op jit(solution)/shard_map/dot_general | solution.py:55
  409.1 2.9 constant_dynamic-slice_fusion.3
  418.4 10.2 %convolution_convert_fusion.3 = bf16[2048,1536]{1,0:T(8,128)(2,1)S(1)} fusion(bf16[2048,1152]{1,0:T(8,128)(2,1)} %get-tuple-element.42, bf16[1536,1152]{1,0:T(8,128)(2,1)S(1)} %bitcast.141), kind=kOutput, calls=%fused_computation.3 | convolution fusion | flops 7250903040 | bytes 14548992 | tf_op jit(solution)/shard_map/dot_general | solution.py:59
  431.0 12.1 %convolution_convert_fusion.2 = bf16[1536,1152]{1,0:T(8,128)(2,1)S(1)} fusion(bf16[2048,1536]{1,0:T(8,128)(2,1)} %constant_dynamic-update-slice_fusion.5.cot_ref, bf16[2048,1152]{1,0:T(8,128)(2,1)} %get-tuple-element.42), kind=kOutput, calls=%fused_computation.2 | convolution fusion | flops 7249526784 | bytes 14548992 | tf_op jit(solution)/shard_map/dot_general | solution.py:55
  446.7 2.7 add_convert_fusion
  453.8 2.6 convert_add_fusion.5
  460.0 33.0 %collective-permute-done.33 = bf16[2,2,2,96,1152]{4,3,2,0,1:T(8,128)(2,1)} collective-permute-done((bf16[2,2,2,96,1152]{4,3,2,0,1:T(8,128)(2,1)}, bf16[2,2,2,96,1152]{4,3,2,0,1:T(8,128)(2,1)}, u32[]{:S(2)}, u32[]{:S(2)}) %collective-permute-start.33) | collective-permute-done | bytes 1769504 | tf_op jit(solution)/shard_map/ppermute | solution.py:74
  495.0 34.9 %collective-permute-done.31 = bf16[2,2,2,96,1152]{4,3,2,0,1:T(8,128)(2,1)} collective-permute-done((bf16[2,2,2,96,1152]{4,3,2,0,1:T(8,128)(2,1)}, bf16[2,2,2,96,1152]{4,3,2,0,1:T(8,128)(2,1)}, u32[]{:S(2)}, u32[]{:S(2)}) %collective-permute-start.31) | collective-permute-done | bytes 1769504 | tf_op jit(solution)/shard_map/ppermute | solution.py:74
  531.8 3.0 collective-permute-start.32
  538.5 47.5 %collective-permute-done.34 = bf16[2,2,96,1152]{3,2,1,0:T(8,128)(2,1)S(1)} collective-permute-done((bf16[2,2,96,1152]{3,2,1,0:T(8,128)(2,1)S(1)}, bf16[2,2,96,1152]{3,2,1,0:T(8,128)(2,1)S(1)}, u32[]{:S(2)}, u32[]{:S(2)}) %collective-permute-start.34) | collective-permute-done | bytes 884768 | tf_op jit(solution)/shard_map/ppermute | solution.py:74
  587.2 17.8 %collective-permute-done.32 = bf16[2,2,96,1152]{3,2,1,0:T(8,128)(2,1)S(1)} collective-permute-done((bf16[2,2,96,1152]{3,2,1,0:T(8,128)(2,1)S(1)}, bf16[2,2,96,1152]{3,2,1,0:T(8,128)(2,1)S(1)}, u32[]{:S(2)}, u32[]{:S(2)}) %collective-permute-start.32) | collective-permute-done | bytes 884768 | tf_op jit(solution)/shard_map/ppermute | solution.py:74
  611.8 2.3 convolution_convert_fusion.6
  614.0 21.1 %attend_back.1 = (bf16[4,128,768]{2,1,0:T(8,128)(2,1)}, bf16[8,4,128,256]{3,2,1,0:T(8,128)(2,1)}) custom-call(bf16[4,128,768]{2,1,0:T(8,128)(2,1)} %copy.56.q_ref, bf16[4,128,768]{2,1,0:T(8,128)(2,1)} %bitcast.181, bf16[8,4,128,256]{3,2,1,0:T(8,128)(2,1)} %shard_map.264.kv_ref, s32[4,128,1]{2,1,0:T(8,128)} %copy.57.sq_ref, s32[4,128,1]{2,1,0:T(8,128)} %copy.58.pq_ref, ...), custom_call_target="tpu_custom_call" | custom-call | flops 4026531840 | bytes 7340032 | tf_op jit(solution)/shard_map/attend_back/pallas_call | solution.py:187
  635.2 37.4 %shard_map.265 = f32[4,128,256]{2,1,0:T(8,128)} custom-call(bf16[8,4,128,256]{3,2,1,0:T(8,128)(2,1)} %get-tuple-element.48.refs_0_), custom_call_target="tpu_custom_call" | custom-call | bytes 100000000 | tf_op jit(solution)/shard_map/pallas_call | solution.py:568
  681.1 5.3 convolution_convert_fusion.4
  686.5 3.1 fusion.10
  692.5 2.8 convolution_convert_fusion.5
  695.3 75.2 %shard_map.266 = (f32[96,1024]{1,0:T(8,128)}, f32[96,768]{1,0:T(8,128)}, f32[32,128]{1,0:T(8,128)}, f32[96,4480]{1,0:T(8,128)}, f32[96,4480]{1,0:T(8,128)}, /*index=5*/f32[96,4480]{1,0:T(8,128)}) custom-call(bf16[16,96,1024]{2,1,0:T(8,128)(2,1)} %bitcast.147, bf16[16,96,768]{2,1,0:T(8,128)(2,1)} %bitcast.152, f32[32,128]{1,0:T(8,128)} %maximum_bitcast_fusion.refs_2_, ...), custom_call_target="tpu_custom_call" | custom-call | bytes 100000000 | tf_op jit(solution)/shard_map/pallas_call | solution.py:568
  777.4 2.8 fusion.27
  780.9 2.9 fusion.15
  783.9 4.2 fusion.14
  788.0 9.8 %collective-permute-done.19 = bf16[256,1536]{1,0:T(8,128)(2,1)S(1)} collective-permute-done((bf16[256,1536]{1,0:T(8,128)(2,1)S(1)}, bf16[256,1536]{1,0:T(8,128)(2,1)S(1)}, u32[]{:S(2)}, u32[]{:S(2)}) %collective-permute-start.19) | collective-permute-done | bytes 786464 | tf_op jit(solution)/shard_map/ppermute | solution.py:74
  (246 shorter events, 99.4 us)
Async XLA Ops:
  0.6 66.9 %copy-start.29 = (s32[4,128]{1,0:T(4,128)S(1)}, s32[4,128]{1,0:T(4,128)}, u32[]{:S(2)}) copy-start(s32[4,128]{1,0:T(4,128)} %param.18) | copy-start | bytes 6148
  0.7 66.9 %copy-start.41 = (bf16[6,128]{1,0:T(8,128)(2,1)S(1)}, bf16[6,128]{1,0:T(8,128)(2,1)}, u32[]{:S(2)}) copy-start(bf16[6,128]{1,0:T(8,128)(2,1)} %param.22) | copy-start | bytes 4612
  0.7 66.9 %copy-start.43 = (bf16[1,128]{1,0:T(2,128)(2,1)S(1)}, bf16[1,128]{1,0:T(2,128)(2,1)}, u32[]{:S(2)}) copy-start(bf16[1,128]{1,0:T(2,128)(2,1)} %param.24) | copy-start | bytes 772
  0.7 66.9 %copy-start.42 = (bf16[1,128]{1,0:T(2,128)(2,1)S(1)}, bf16[1,128]{1,0:T(2,128)(2,1)}, u32[]{:S(2)}) copy-start(bf16[1,128]{1,0:T(2,128)(2,1)} %param.26) | copy-start | bytes 772
  66.0 101.9 %collective-permute-start.1 = (bf16[1536,768]{1,0:T(8,128)(2,1)}, bf16[1536,768]{1,0:T(8,128)(2,1)}, u32[]{:S(2)}, u32[]{:S(2)}) collective-permute-start(bf16[1536,768]{1,0:T(8,128)(2,1)} %bitcast.150), channel_id=1, source_target_pairs={{0,1},{1,0},{2,3},{3,2},{4,5},{5,4},{6,7},{7,6},{8,9},{9,8},{10,11... | collective-permute-start | bytes 7077896 | tf_op jit(solution)/shard_map/ppermute | solution.py:74
  67.5 176.9 %copy-start.37 = (f32[64]{0:T(128)}, f32[64]{0:T(128)S(1)}, u32[]{:S(2)}) copy-start(f32[64]{0:T(128)S(1)} %multiply_power_fusion) | copy-start | bytes 772
  74.1 37.6 %copy-start.30 = (s32[4,128]{1,0:T(4,128)S(1)}, s32[4,128]{1,0:T(4,128)}, u32[]{:S(2)}) copy-start(s32[4,128]{1,0:T(4,128)} %param.17) | copy-start | bytes 6148
  127.4 18.7 %collective-permute-start = (bf16[512,768]{1,0:T(8,128)(2,1)}, bf16[512,768]{1,0:T(8,128)(2,1)}, u32[]{:S(2)}, u32[]{:S(2)}) collective-permute-start(bf16[512,768]{1,0:T(8,128)(2,1)} %bitcast.161), channel_id=1, source_target_pairs={{0,1},{1,0},{2,3},{3,2},{4,5},{5,4},{6,7},{7,6},{8,9},{9,8},{10,11... | collective-permute-start | bytes 2359304 | tf_op jit(solution)/shard_map/ppermute | solution.py:74
  129.9 37.9 %copy-start.11 = (bf16[16,96,768]{2,1,0:T(8,128)(2,1)S(1)}, bf16[16,96,768]{2,1,0:T(8,128)(2,1)}, u32[]{:S(2)}) copy-start(bf16[16,96,768]{2,1,0:T(8,128)(2,1)} %get-tuple-element.39) | copy-start | bytes 7077892
  131.3 33.6 %collective-permute-start.21 = (bf16[256,1536]{1,0:T(8,128)(2,1)S(1)}, bf16[256,1536]{1,0:T(8,128)(2,1)}, u32[]{:S(2)}, u32[]{:S(2)}) collective-permute-start(bf16[256,1536]{1,0:T(8,128)(2,1)S(1)} %constant_dynamic-slice_fusion.8), channel_id=1, source_target_pairs={{0,4},{2,6},{4,0},{6,2},{8,12},{10,14},{12,8},{14,10},{1,5},{3,7},... | collective-permute-start | bytes 2359304 | tf_op jit(solution)/shard_map/ppermute | solution.py:74
  132.4 74.3 %collective-permute-start.7 = (bf16[4,96,1152]{2,1,0:T(8,128)(2,1)}, bf16[4,96,1152]{2,1,0:T(8,128)(2,1)}, u32[]{:S(2)}, u32[]{:S(2)}) collective-permute-start(bf16[4,96,1152]{2,1,0:T(8,128)(2,1)} %get-tuple-element.40.refs_0_), channel_id=1, source_target_pairs={{0,8},{2,10},{4,12},{6,14},{8,0},{10,2},{12,4},{14,6},{1,9},{3,11}... | collective-permute-start | bytes 2654216 | tf_op jit(solution)/shard_map/ppermute | solution.py:74
  133.9 89.9 %collective-permute-start.6 = (bf16[4,96,1152]{2,1,0:T(8,128)(2,1)}, bf16[4,96,1152]{2,1,0:T(8,128)(2,1)}, u32[]{:S(2)}, u32[]{:S(2)}) collective-permute-start(bf16[4,96,1152]{2,1,0:T(8,128)(2,1)} %get-tuple-element.40.refs_0_), channel_id=1, source_target_pairs={{0,2},{2,0},{4,6},{6,4},{8,10},{10,8},{12,14},{14,12},{1,3},{3,1},... | collective-permute-start | bytes 2654216 | tf_op jit(solution)/shard_map/ppermute | solution.py:74
  134.3 39.0 %copy-start.23 = (f32[1536]{0:T(1024)}, f32[1536]{0:T(1024)S(1)}, u32[]{:S(2)}) copy-start(f32[1536]{0:T(1024)S(1)} %convert_element_type.229) | copy-start | bytes 18436
  146.1 27.8 %collective-permute-start.20 = (bf16[512,1536]{1,0:T(8,128)(2,1)}, bf16[512,1536]{1,0:T(8,128)(2,1)S(1)}, u32[]{:S(2)}, u32[]{:S(2)}) collective-permute-start(bf16[512,1536]{1,0:T(8,128)(2,1)} %get-tuple-element.122), channel_id=1, source_target_pairs={{0,16},{16,0},{1,17},{17,1},{2,18},{18,2},{3,19},{19,3},{4,20},{20... | collective-permute-start | bytes 4718600 | tf_op jit(solution)/shard_map/ppermute | solution.py:74
  164.9 17.9 %collective-permute-start.22 = (bf16[256,1536]{1,0:T(8,128)(2,1)}, bf16[256,1536]{1,0:T(8,128)(2,1)S(1)}, u32[]{:S(2)}, u32[]{:S(2)}) collective-permute-start(bf16[256,1536]{1,0:T(8,128)(2,1)} %collective-permute-done.21), channel_id=1, source_target_pairs={{0,1},{1,0},{2,3},{3,2},{4,5},{5,4},{6,7},{7,6},{8,9},{9,8},{10,11... | collective-permute-start | bytes 2359304 | tf_op jit(solution)/shard_map/ppermute | solution.py:74
  173.7 32.8 %collective-permute-start.2 = (bf16[512,1536]{1,0:T(8,128)(2,1)S(1)}, bf16[512,1536]{1,0:T(8,128)(2,1)S(1)}, u32[]{:S(2)}, u32[]{:S(2)}) collective-permute-start(bf16[512,1536]{1,0:T(8,128)(2,1)S(1)} %get-tuple-element.69), channel_id=1, source_target_pairs={{0,16},{16,0},{1,17},{17,1},{2,18},{18,2},{3,19},{19,3},{4,20},{20... | collective-permute-start | bytes 4718600 | tf_op jit(solution)/shard_map/ppermute | solution.py:74
  173.9 30.3 %collective-permute-start.3 = (bf16[256,1536]{1,0:T(8,128)(2,1)S(1)}, bf16[256,1536]{1,0:T(8,128)(2,1)S(1)}, u32[]{:S(2)}, u32[]{:S(2)}) collective-permute-start(bf16[256,1536]{1,0:T(8,128)(2,1)S(1)} %constant_dynamic-slice_fusion.9), channel_id=1, source_target_pairs={{0,4},{2,6},{4,0},{6,2},{8,12},{10,14},{12,8},{14,10},{1,5},{3,7},... | collective-permute-start | bytes 2359304 | tf_op jit(solution)/shard_map/ppermute | solution.py:74
  182.7 61.7 %collective-permute-start.10 = (bf16[4,96,1152]{2,1,0:T(8,128)(2,1)}, bf16[4,96,1152]{2,1,0:T(8,128)(2,1)}, u32[]{:S(2)}, u32[]{:S(2)}) collective-permute-start(bf16[4,96,1152]{2,1,0:T(8,128)(2,1)} %get-tuple-element.41.refs_0_), channel_id=1, source_target_pairs={{0,8},{2,10},{4,12},{6,14},{8,0},{10,2},{12,4},{14,6},{1,9},{3,11}... | collective-permute-start | bytes 2654216 | tf_op jit(solution)/shard_map/ppermute | solution.py:74
  204.1 19.2 %collective-permute-start.4 = (bf16[256,1536]{1,0:T(8,128)(2,1)S(1)}, bf16[256,1536]{1,0:T(8,128)(2,1)S(1)}, u32[]{:S(2)}, u32[]{:S(2)}) collective-permute-start(bf16[256,1536]{1,0:T(8,128)(2,1)S(1)} %collective-permute-done.3), channel_id=1, source_target_pairs={{0,1},{1,0},{2,3},{3,2},{4,5},{5,4},{6,7},{7,6},{8,9},{9,8},{10,11... | collective-permute-start | bytes 2359304 | tf_op jit(solution)/shard_map/ppermute | solution.py:74
  206.5 39.9 %collective-permute-start.9 = (bf16[4,96,1152]{2,1,0:T(8,128)(2,1)}, bf16[4,96,1152]{2,1,0:T(8,128)(2,1)}, u32[]{:S(2)}, u32[]{:S(2)}) collective-permute-start(bf16[4,96,1152]{2,1,0:T(8,128)(2,1)} %get-tuple-element.41.refs_0_), channel_id=1, source_target_pairs={{0,2},{2,0},{4,6},{6,4},{8,10},{10,8},{12,14},{14,12},{1,3},{3,1},... | collective-permute-start | bytes 2654216 | tf_op jit(solution)/shard_map/ppermute | solution.py:74
  206.7 53.1 %collective-permute-start.13 = (bf16[4,96,1152]{2,1,0:T(8,128)(2,1)}, bf16[4,96,1152]{2,1,0:T(8,128)(2,1)}, u32[]{:S(2)}, u32[]{:S(2)}) collective-permute-start(bf16[4,96,1152]{2,1,0:T(8,128)(2,1)} %get-tuple-element.43.refs_0_), channel_id=1, source_target_pairs={{0,8},{2,10},{4,12},{6,14},{8,0},{10,2},{12,4},{14,6},{1,9},{3,11}... | collective-permute-start | bytes 2654216 | tf_op jit(solution)/shard_map/ppermute | solution.py:74
  223.3 40.3 %collective-permute-start.8 = (bf16[4,96,1152]{2,1,0:T(8,128)(2,1)}, bf16[4,96,1152]{2,1,0:T(8,128)(2,1)}, u32[]{:S(2)}, u32[]{:S(2)}) collective-permute-start(bf16[4,96,1152]{2,1,0:T(8,128)(2,1)} %collective-permute-done.7.refs_2_), channel_id=1, source_target_pairs={{0,2},{2,0},{4,6},{6,4},{8,10},{10,8},{12,14},{14,12},{1,3},{3,1},... | collective-permute-start | bytes 2654216 | tf_op jit(solution)/shard_map/ppermute | solution.py:74
  223.8 39.9 %copy-start.33 = (bf16[1536]{0:T(1024)(128)(2,1)S(1)}, bf16[1536]{0:T(1024)(128)(2,1)}, u32[]{:S(2)}) copy-start(bf16[1536]{0:T(1024)(128)(2,1)} %param.20) | copy-start | bytes 9220
  223.8 88.1 %collective-permute-start.23 = (bf16[512,1536]{1,0:T(8,128)(2,1)}, bf16[512,1536]{1,0:T(8,128)(2,1)}, u32[]{:S(2)}, u32[]{:S(2)}) collective-permute-start(bf16[512,1536]{1,0:T(8,128)(2,1)} %pad_maximum_fusion.4), channel_id=1, source_target_pairs={{0,16},{16,0},{1,17},{17,1},{2,18},{18,2},{3,19},{19,3},{4,20},{20... | collective-permute-start | bytes 4718600 | tf_op jit(solution)/shard_map/ppermute | solution.py:74
  244.4 70.1 %collective-permute-start.5 = (bf16[512,1536]{1,0:T(8,128)(2,1)}, bf16[512,1536]{1,0:T(8,128)(2,1)}, u32[]{:S(2)}, u32[]{:S(2)}) collective-permute-start(bf16[512,1536]{1,0:T(8,128)(2,1)} %pad_maximum_fusion.1), channel_id=1, source_target_pairs={{0,16},{16,0},{1,17},{17,1},{2,18},{18,2},{3,19},{19,3},{4,20},{20... | collective-permute-start | bytes 4718600 | tf_op jit(solution)/shard_map/ppermute | solution.py:74
  246.4 25.0 %collective-permute-start.11 = (bf16[4,96,1152]{2,1,0:T(8,128)(2,1)}, bf16[4,96,1152]{2,1,0:T(8,128)(2,1)}, u32[]{:S(2)}, u32[]{:S(2)}) collective-permute-start(bf16[4,96,1152]{2,1,0:T(8,128)(2,1)} %collective-permute-done.10.refs_2_), channel_id=1, source_target_pairs={{0,2},{2,0},{4,6},{6,4},{8,10},{10,8},{12,14},{14,12},{1,3},{3,1},... | collective-permute-start | bytes 2654216 | tf_op jit(solution)/shard_map/ppermute | solution.py:74
  259.8 29.6 %collective-permute-start.12 = (bf16[4,96,1152]{2,1,0:T(8,128)(2,1)}, bf16[4,96,1152]{2,1,0:T(8,128)(2,1)}, u32[]{:S(2)}, u32[]{:S(2)}) collective-permute-start(bf16[4,96,1152]{2,1,0:T(8,128)(2,1)} %get-tuple-element.43.refs_0_), channel_id=1, source_target_pairs={{0,2},{2,0},{4,6},{6,4},{8,10},{10,8},{12,14},{14,12},{1,3},{3,1},... | collective-permute-start | bytes 2654216 | tf_op jit(solution)/shard_map/ppermute | solution.py:74
  263.7 44.6 %collective-permute-start.14 = (bf16[4,96,1152]{2,1,0:T(8,128)(2,1)}, bf16[4,96,1152]{2,1,0:T(8,128)(2,1)}, u32[]{:S(2)}, u32[]{:S(2)}) collective-permute-start(bf16[4,96,1152]{2,1,0:T(8,128)(2,1)} %collective-permute-done.13.refs_2_), channel_id=1, source_target_pairs={{0,2},{2,0},{4,6},{6,4},{8,10},{10,8},{12,14},{14,12},{1,3},{3,1},... | collective-permute-start | bytes 2654216 | tf_op jit(solution)/shard_map/ppermute | solution.py:74
  413.3 44.8 %collective-permute-start.35 = (bf16[2,2,2,96,1152]{4,3,2,0,1:T(8,128)(2,1)}, bf16[2,2,2,96,1152]{4,3,2,0,1:T(8,128)(2,1)S(1)}, u32[]{:S(2)}, u32[]{:S(2)}) collective-permute-start(bf16[2,2,2,96,1152]{4,3,2,0,1:T(8,128)(2,1)} %bitcast.129), channel_id=1, source_target_pairs={{0,2},{2,0},{4,6},{6,4},{8,10},{10,8},{12,14},{14,12},{1,3},{3,1},... | collective-permute-start | bytes 5308424 | tf_op jit(solution)/shard_map/ppermute | solution.py:74
  416.6 28.1 %collective-permute-start.24 = (bf16[512,1536]{1,0:T(8,128)(2,1)S(1)}, bf16[512,1536]{1,0:T(8,128)(2,1)}, u32[]{:S(2)}, u32[]{:S(2)}) collective-permute-start(bf16[512,1536]{1,0:T(8,128)(2,1)S(1)} %get-tuple-element.73), channel_id=1, source_target_pairs={{0,16},{16,0},{1,17},{17,1},{2,18},{18,2},{3,19},{19,3},{4,20},{20... | collective-permute-start | bytes 4718600 | tf_op jit(solution)/shard_map/ppermute | solution.py:74
  416.7 28.3 %collective-permute-start.25 = (bf16[512,1536]{1,0:T(8,128)(2,1)S(1)}, bf16[512,1536]{1,0:T(8,128)(2,1)}, u32[]{:S(2)}, u32[]{:S(2)}) collective-permute-start(bf16[512,1536]{1,0:T(8,128)(2,1)S(1)} %get-tuple-element.72), channel_id=1, source_target_pairs={{0,16},{16,0},{1,17},{17,1},{2,18},{18,2},{3,19},{19,3},{4,20},{20... | collective-permute-start | bytes 4718600 | tf_op jit(solution)/shard_map/ppermute | solution.py:74
  430.5 20.2 %collective-permute-start.15 = (bf16[512,1536]{1,0:T(8,128)(2,1)}, bf16[512,1536]{1,0:T(8,128)(2,1)S(1)}, u32[]{:S(2)}, u32[]{:S(2)}) collective-permute-start(bf16[512,1536]{1,0:T(8,128)(2,1)} %get-tuple-element.76), channel_id=1, source_target_pairs={{0,16},{16,0},{1,17},{17,1},{2,18},{18,2},{3,19},{19,3},{4,20},{20... | collective-permute-start | bytes 4718600 | tf_op jit(solution)/shard_map/ppermute | solution.py:74
  430.5 20.2 %collective-permute-start.16 = (bf16[512,1536]{1,0:T(8,128)(2,1)}, bf16[512,1536]{1,0:T(8,128)(2,1)S(1)}, u32[]{:S(2)}, u32[]{:S(2)}) collective-permute-start(bf16[512,1536]{1,0:T(8,128)(2,1)} %get-tuple-element.77), channel_id=1, source_target_pairs={{0,16},{16,0},{1,17},{17,1},{2,18},{18,2},{3,19},{19,3},{4,20},{20... | collective-permute-start | bytes 4718600 | tf_op jit(solution)/shard_map/ppermute | solution.py:74
  444.7 48.3 %collective-permute-start.33 = (bf16[2,2,2,96,1152]{4,3,2,0,1:T(8,128)(2,1)}, bf16[2,2,2,96,1152]{4,3,2,0,1:T(8,128)(2,1)}, u32[]{:S(2)}, u32[]{:S(2)}) collective-permute-start(bf16[2,2,2,96,1152]{4,3,2,0,1:T(8,128)(2,1)} %bitcast.130), channel_id=1, source_target_pairs={{0,2},{2,0},{4,6},{6,4},{8,10},{10,8},{12,14},{14,12},{1,3},{3,1},... | collective-permute-start | bytes 5308424 | tf_op jit(solution)/shard_map/ppermute | solution.py:74
  445.0 84.9 %collective-permute-start.31 = (bf16[2,2,2,96,1152]{4,3,2,0,1:T(8,128)(2,1)}, bf16[2,2,2,96,1152]{4,3,2,0,1:T(8,128)(2,1)}, u32[]{:S(2)}, u32[]{:S(2)}) collective-permute-start(bf16[2,2,2,96,1152]{4,3,2,0,1:T(8,128)(2,1)} %bitcast.131), channel_id=1, source_target_pairs={{0,2},{2,0},{4,6},{6,4},{8,10},{10,8},{12,14},{14,12},{1,3},{3,1},... | collective-permute-start | bytes 5308424 | tf_op jit(solution)/shard_map/ppermute | solution.py:74
  450.7 81.1 %collective-permute-start.26 = (bf16[256,1536]{1,0:T(8,128)(2,1)}, bf16[256,1536]{1,0:T(8,128)(2,1)S(1)}, u32[]{:S(2)}, u32[]{:S(2)}) collective-permute-start(bf16[256,1536]{1,0:T(8,128)(2,1)} %get-tuple-element.94), channel_id=1, source_target_pairs={{0,4},{2,6},{4,0},{6,2},{8,12},{10,14},{12,8},{14,10},{1,5},{3,7},... | collective-permute-start | bytes 2359304 | tf_op jit(solution)/shard_map/ppermute | solution.py:74
  452.3 82.5 %collective-permute-start.28 = (bf16[256,1536]{1,0:T(8,128)(2,1)}, bf16[256,1536]{1,0:T(8,128)(2,1)S(1)}, u32[]{:S(2)}, u32[]{:S(2)}) collective-permute-start(bf16[256,1536]{1,0:T(8,128)(2,1)} %get-tuple-element.95), channel_id=1, source_target_pairs={{0,4},{2,6},{4,0},{6,2},{8,12},{10,14},{12,8},{14,10},{1,5},{3,7},... | collective-permute-start | bytes 2359304 | tf_op jit(solution)/shard_map/ppermute | solution.py:74
  458.1 148.0 %collective-permute-start.17 = (bf16[512,1536]{1,0:T(8,128)(2,1)S(1)}, bf16[512,1536]{1,0:T(8,128)(2,1)S(1)}, u32[]{:S(2)}, u32[]{:S(2)}) collective-permute-start(bf16[512,1536]{1,0:T(8,128)(2,1)S(1)} %pad_maximum_fusion.2), channel_id=1, source_target_pairs={{0,1},{1,0},{2,3},{3,2},{4,5},{5,4},{6,7},{7,6},{8,9},{9,8},{10,11... | collective-permute-start | bytes 4718600 | tf_op jit(solution)/shard_map/ppermute | solution.py:74
  493.0 43.8 %collective-permute-start.36 = (bf16[2,2,96,1152]{3,2,1,0:T(8,128)(2,1)S(1)}, bf16[2,2,96,1152]{3,2,1,0:T(8,128)(2,1)S(1)}, u32[]{:S(2)}, u32[]{:S(2)}) collective-permute-start(bf16[2,2,96,1152]{3,2,1,0:T(8,128)(2,1)S(1)} %fusion.33), channel_id=1, source_target_pairs={{0,8},{2,10},{4,12},{6,14},{8,0},{10,2},{12,4},{14,6},{1,9},{3,11}... | collective-permute-start | bytes 2654216 | tf_op jit(solution)/shard_map/ppermute | solution.py:74
  529.9 56.2 %collective-permute-start.34 = (bf16[2,2,96,1152]{3,2,1,0:T(8,128)(2,1)S(1)}, bf16[2,2,96,1152]{3,2,1,0:T(8,128)(2,1)S(1)}, u32[]{:S(2)}, u32[]{:S(2)}) collective-permute-start(bf16[2,2,96,1152]{3,2,1,0:T(8,128)(2,1)S(1)} %fusion.32), channel_id=1, source_target_pairs={{0,8},{2,10},{4,12},{6,14},{8,0},{10,2},{12,4},{14,6},{1,9},{3,11}... | collective-permute-start | bytes 2654216 | tf_op jit(solution)/shard_map/ppermute | solution.py:74
  531.8 73.1 %collective-permute-start.32 = (bf16[2,2,96,1152]{3,2,1,0:T(8,128)(2,1)S(1)}, bf16[2,2,96,1152]{3,2,1,0:T(8,128)(2,1)S(1)}, u32[]{:S(2)}, u32[]{:S(2)}) collective-permute-start(bf16[2,2,96,1152]{3,2,1,0:T(8,128)(2,1)S(1)} %fusion.31), channel_id=1, source_target_pairs={{0,8},{2,10},{4,12},{6,14},{8,0},{10,2},{12,4},{14,6},{1,9},{3,11}... | collective-permute-start | bytes 2654216 | tf_op jit(solution)/shard_map/ppermute | solution.py:74
  535.3 72.5 %collective-permute-start.27 = (bf16[256,1536]{1,0:T(8,128)(2,1)S(1)}, bf16[256,1536]{1,0:T(8,128)(2,1)S(1)}, u32[]{:S(2)}, u32[]{:S(2)}) collective-permute-start(bf16[256,1536]{1,0:T(8,128)(2,1)S(1)} %get-tuple-element.88), channel_id=1, source_target_pairs={{0,1},{1,0},{2,3},{3,2},{4,5},{5,4},{6,7},{7,6},{8,9},{9,8},{10,11... | collective-permute-start | bytes 2359304 | tf_op jit(solution)/shard_map/ppermute | solution.py:74
  536.9 71.5 %collective-permute-start.29 = (bf16[256,1536]{1,0:T(8,128)(2,1)S(1)}, bf16[256,1536]{1,0:T(8,128)(2,1)S(1)}, u32[]{:S(2)}, u32[]{:S(2)}) collective-permute-start(bf16[256,1536]{1,0:T(8,128)(2,1)S(1)} %get-tuple-element.89), channel_id=1, source_target_pairs={{0,1},{1,0},{2,3},{3,2},{4,5},{5,4},{6,7},{7,6},{8,9},{9,8},{10,11... | collective-permute-start | bytes 2359304 | tf_op jit(solution)/shard_map/ppermute | solution.py:74
  607.8 169.6 %collective-permute-start.18 = (bf16[256,1536]{1,0:T(8,128)(2,1)}, bf16[256,1536]{1,0:T(8,128)(2,1)}, u32[]{:S(2)}, u32[]{:S(2)}) collective-permute-start(bf16[256,1536]{1,0:T(8,128)(2,1)} %fusion.24), channel_id=1, source_target_pairs={{0,4},{2,6},{4,0},{6,2},{8,12},{10,14},{12,8},{14,10},{1,5},{3,7},... | collective-permute-start | bytes 2359304 | tf_op jit(solution)/shard_map/ppermute | solution.py:74
  635.1 42.7 %copy-start.28 = (f32[512]{0:T(512)S(1)}, f32[512]{0:T(512)}, u32[]{:S(2)}) copy-start(f32[512]{0:T(512)} %copy-done.27) | copy-start | bytes 6148
  635.2 42.6 %copy-start.38 = (f32[64]{0:T(128)S(1)}, f32[64]{0:T(128)}, u32[]{:S(2)}) copy-start(f32[64]{0:T(128)} %copy-done.37) | copy-start | bytes 772
  689.6 91.4 %collective-permute-start.30 = (bf16[512,1536]{1,0:T(8,128)(2,1)}, bf16[512,1536]{1,0:T(8,128)(2,1)}, u32[]{:S(2)}, u32[]{:S(2)}) collective-permute-start(bf16[512,1536]{1,0:T(8,128)(2,1)} %get-tuple-element.87), channel_id=1, source_target_pairs={{0,1},{1,0},{2,3},{3,2},{4,5},{5,4},{6,7},{7,6},{8,9},{9,8},{10,11... | collective-permute-start | bytes 4718600 | tf_op jit(solution)/shard_map/ppermute | solution.py:74
  780.2 17.6 %collective-permute-start.19 = (bf16[256,1536]{1,0:T(8,128)(2,1)S(1)}, bf16[256,1536]{1,0:T(8,128)(2,1)S(1)}, u32[]{:S(2)}, u32[]{:S(2)}) collective-permute-start(bf16[256,1536]{1,0:T(8,128)(2,1)S(1)} %fusion.27), channel_id=1, source_target_pairs={{0,1},{1,0},{2,3},{3,2},{4,5},{5,4},{6,7},{7,6},{8,9},{9,8},{10,11... | collective-permute-start | bytes 2359304 | tf_op jit(solution)/shard_map/ppermute | solution.py:74
  (37 other events, 173.4 us)
